TPU v7x, 256 devices: a whole 4x4x8 slice. The times are simulated.
256 devices in a mesh: shock: 32 (over z, x_lo, core), trans: 8 (over x_hi, y).
Axes of the slice: x: 4 (x_hi: 2, x_lo: 2; x = x_hi * 2 + x_lo), y: 4, z: 8, core: 2. Of those that a mesh axis runs over, the one named last changes fastest.
Arguments:
- displacement: float32 [3, 65536], P(None, ('shock', 'trans')), may hold values from -0.32 to 0.32
- velocity: float32 [3, 65536], P(None, ('shock', 'trans')), may hold values from -4 to 4
- force_before: float32 [3, 65536], P(None, ('shock', 'trans')), may hold values from -4 to 4
- beta: float32 [50], replicated, may hold values from -0.875 to 0.875
- alpha: float32 [50, 50], replicated, may hold values from -0.125 to 0.125
- live_count: int32 [256], P(('shock', 'trans')), may hold values from 128 to 256, as said below
- trans_send: int32 [2, 8192], P(None, ('shock', 'trans')), may hold values from 0 to 127, as said below
- shock_send: int32 [2, 32768], P(None, ('shock', 'trans')), may hold values from 0 to 319, as said below
- neighbour_block: int32 [26, 65536], P(None, ('shock', 'trans')), may hold values from -1 to 4, as said below
- neighbour_lane: int32 [26, 65536], P(None, ('shock', 'trans')), may hold values from 0 to 127, as said below
- leaving_slots: int32 [4096], P(('shock', 'trans')), may hold values from 0 to 127, as said below
- leaving_count: int32 [256], P(('shock', 'trans')), may hold values from 8 to 16, as said below
Outputs:
- displacement_next: float32 [3, 65536], P(None, ('shock', 'trans'))
- velocity_next: float32 [3, 65536], P(None, ('shock', 'trans'))
- force_next: float32 [3, 65536], P(None, ('shock', 'trans'))
- atom_energy: float32 [65536], P(('shock', 'trans'))
- arrivals: float32 [3, 3, 4096], P(None, None, ('shock', 'trans'))
Inputs may be any that keep to these rules, and one draw needn't show every extreme that they name: A store's live atoms are its slots 0 to live_count - 1; stores at the lowest shock indices, behind the front, are full, and some store holds 256. `trans_send`: entries are live atoms of the sending store. `shock_send`: entries are live atoms or transverse ghost columns of the sending store's first section. `neighbour_block`: -1 marks an absent neighbour; slots at or above live_count have none; otherwise the column names a live own atom or a ghost column, never a ghost block beyond an open end of the shock axis. `neighbour_lane`: read together with neighbour_block. `leaving_slots`: distinct live atoms of the store. `leaving_count`: some store uses all 16 entries.
All inputs are finite; a program needn't handle non-finite values.
Results may differ from a plain program's by a relative error of at most 0.0003.
Values sent between devices are 32-bit elements; how exact they have to be, the bound alone decides.
A program may use at most 64 MiB of HBM per device.

v0:
```python
import math

import jax
import jax.numpy as jnp
import numpy as np
from jax import lax
from jax.sharding import PartitionSpec as P

kick_factor = 0.5
drift_step = 0.02
cutoff_radius = 4.2
radial_width = 0.35
radial_centers = (1.4, 1.9, 2.4, 2.9)
moment_scale = 0.25
pair_list = ((0, 0), (0, 1), (0, 2), (0, 3), (1, 1), (1, 2), (1, 3), (2, 2), (2, 3), (3, 3))
highest = lax.Precision.HIGHEST


def from_behind(block, axis, distance):
    devices = range(lax.axis_size(axis))
    route = [((i - distance) % len(devices), i) for i in devices]
    return lax.ppermute(block, axis, route)


def passed_along(x, axis, by):
    devices = lax.axis_size(axis)
    pairs = [(i, i + by) for i in range(devices) if 0 <= i + by < devices]
    return lax.ppermute(x, axis, pairs)


def lattice_table():
    entries = []
    for number in range(8):
        entries.append(
            [1.0 - 2.0 * (number >> 2 & 1), 1.0 - 2.0 * (number >> 1 & 1), 1.0 - 2.0 * (number & 1)]
        )
    for axis_pick in range(3):
        for signed in (2.0, -2.0):
            vector = [0.0, 0.0, 0.0]
            vector[axis_pick] = signed
            entries.append(vector)
    for zero_pick in (2, 1, 0):
        others = [axis_pick for axis_pick in range(3) if axis_pick != zero_pick]
        for leading in (2.0, -2.0):
            for trailing in (2.0, -2.0):
                vector = [0.0, 0.0, 0.0]
                vector[others[0]] = leading
                vector[others[1]] = trailing
                entries.append(vector)
    return np.array(entries, dtype=np.float32).T


def exponent_table():
    triples = []
    for degree in range(5):
        for first_power in range(degree, -1, -1):
            for second_power in range(degree - first_power, -1, -1):
                triples.append(
                    (degree, first_power, second_power, degree - first_power - second_power)
                )
    return triples


def contraction_weights():
    triples = exponent_table()
    matrix = np.zeros((5, len(triples)), dtype=np.float32)
    for column, (degree, first_power, second_power, third_power) in enumerate(triples):
        matrix[degree, column] = math.factorial(degree) / (
            math.factorial(first_power) * math.factorial(second_power) * math.factorial(third_power)
        )
    return matrix


def block_energy(vectors, present, beta, alpha):
    distance = jnp.sqrt(jnp.sum(vectors * vectors, axis=0))
    direction = vectors / distance[None]
    smooth = 0.5 * (jnp.cos(jnp.pi * distance / cutoff_radius) + 1.0) * present
    radial = jnp.stack(
        [
            smooth * jnp.exp(-jnp.square((distance - center) / radial_width))
            for center in radial_centers
        ]
    )
    powers_first = [jnp.ones_like(distance)]
    powers_second = [jnp.ones_like(distance)]
    powers_third = [jnp.ones_like(distance)]
    for degree in range(4):
        powers_first.append(powers_first[-1] * direction[0])
        powers_second.append(powers_second[-1] * direction[1])
        powers_third.append(powers_third[-1] * direction[2])
    monomials = jnp.stack(
        [
            powers_first[first_power] * powers_second[second_power] * powers_third[third_power]
            for degree, first_power, second_power, third_power in exponent_table()
        ]
    )
    moments = moment_scale * jnp.einsum("nkb,mkb->nmb", radial, monomials, precision=highest)
    products = jnp.stack(
        [moments[first_index] * moments[second_index] for first_index, second_index in pair_list]
    )
    weights = jnp.asarray(contraction_weights())
    descriptor = jnp.einsum("lm,pmb->plb", weights, products, precision=highest)
    descriptor = descriptor.reshape(len(pair_list) * 5, descriptor.shape[2])
    linear = jnp.dot(beta, descriptor, precision=highest)
    quadratic = jnp.sum(descriptor * jnp.dot(alpha, descriptor, precision=highest), axis=0)
    return linear + 0.5 * quadratic


def store_terms(extended, own_rows, neighbour_block, neighbour_lane, beta, alpha):
    slot_count = own_rows.shape[1]
    block_rows = min(slot_count, 2048)
    groups = slot_count // block_rows
    offsets = jnp.asarray(lattice_table())
    present = neighbour_block >= 0
    clamped = jnp.where(present, neighbour_block * 128 + neighbour_lane, 0)
    weight_live = present.astype(extended.dtype)

    def one_group(inputs):
        clamped_rows, live_rows, own_group = inputs
        vectors = offsets[:, :, None] + extended[:, clamped_rows] - own_group[:, None, :]
        energies, pullback = jax.vjp(
            lambda moved: block_energy(moved, live_rows, beta, alpha), vectors
        )
        (pair_grad,) = pullback(jnp.ones_like(energies))
        return (energies, pair_grad)

    def grouped(array):
        return jnp.moveaxis(array.reshape(array.shape[:-1] + (groups, block_rows)), -2, 0)

    energies, pair_grad = lax.map(
        one_group, (grouped(clamped), grouped(weight_live), grouped(own_rows))
    )
    energies = energies.reshape(slot_count)
    pair_grad = jnp.moveaxis(pair_grad, 0, -2).reshape(3, clamped.shape[0], slot_count)
    total = jnp.zeros((3, extended.shape[1]), extended.dtype)
    total = total.at[:, clamped.reshape(-1)].add(pair_grad.reshape(3, -1))
    total = total.at[:, :slot_count].add(-jnp.sum(pair_grad, axis=1))
    return (energies, total)


def shards(
    displacement,
    velocity,
    force_before,
    beta,
    alpha,
    live_count,
    trans_send,
    shock_send,
    neighbour_block,
    neighbour_lane,
    leaving_slots,
    leaving_count,
):
    slot_count = displacement.shape[1]
    trans_width = trans_send.shape[1]
    shock_width = shock_send.shape[1]
    half_velocity = velocity + kick_factor * force_before
    displaced = displacement + drift_step * half_velocity
    toward_lower = displaced[:, trans_send[0]]
    toward_upper = displaced[:, trans_send[1]]
    from_lower = from_behind(toward_upper, "trans", 1)
    from_upper = from_behind(toward_lower, "trans", -1)
    first_section = jnp.concatenate([displaced, from_lower, from_upper], axis=1)
    toward_lower = first_section[:, shock_send[0]]
    toward_upper = first_section[:, shock_send[1]]
    from_lower = passed_along(toward_upper, "shock", 1)
    from_upper = passed_along(toward_lower, "shock", -1)
    extended = jnp.concatenate([first_section, from_lower, from_upper], axis=1)
    energies, gradient = store_terms(
        extended, displaced, neighbour_block, neighbour_lane, beta, alpha
    )
    ghost_start = first_section.shape[1]
    lower_ghosts = gradient[:, ghost_start : ghost_start + shock_width]
    upper_ghosts = gradient[:, ghost_start + shock_width :]
    back_lower = passed_along(upper_ghosts, "shock", 1)
    back_upper = passed_along(lower_ghosts, "shock", -1)
    first_grad = (
        gradient[:, :ghost_start]
        .at[:, shock_send[0]]
        .add(back_lower)
        .at[:, shock_send[1]]
        .add(back_upper)
    )
    lower_trans = first_grad[:, slot_count : slot_count + trans_width]
    upper_trans = first_grad[:, slot_count + trans_width :]
    back_lower = from_behind(upper_trans, "trans", 1)
    back_upper = from_behind(lower_trans, "trans", -1)
    own_grad = (
        first_grad[:, :slot_count]
        .at[:, trans_send[0]]
        .add(back_lower)
        .at[:, trans_send[1]]
        .add(back_upper)
    )
    force_new = -own_grad
    velocity_new = half_velocity + kick_factor * force_new
    leave_index = lax.iota(jnp.int32, leaving_slots.shape[0])
    sending = leave_index < leaving_count[0]
    payload = jnp.stack(
        [displaced[:, leaving_slots], velocity_new[:, leaving_slots], force_new[:, leaving_slots]]
    ) * sending.astype(jnp.float32)
    arrivals = passed_along(payload, "shock", -1)
    departed = (
        jnp.zeros((slot_count + 1,), jnp.float32)
        .at[jnp.where(sending, leaving_slots, slot_count)]
        .set(1.0)[:slot_count]
    )
    retained = (lax.iota(jnp.int32, slot_count) < live_count[0]).astype(jnp.float32) * (
        1.0 - departed
    )
    return (
        displaced * retained,
        velocity_new * retained,
        force_new * retained,
        energies * retained,
        arrivals,
    )


def solution(mesh):
    in_specs = (
        P(None, ("shock", "trans")),
        P(None, ("shock", "trans")),
        P(None, ("shock", "trans")),
        P(),
        P(),
        P(("shock", "trans")),
        P(None, ("shock", "trans")),
        P(None, ("shock", "trans")),
        P(None, ("shock", "trans")),
        P(None, ("shock", "trans")),
        P(("shock", "trans")),
        P(("shock", "trans")),
    )
    out_specs = (
        P(None, ("shock", "trans")),
        P(None, ("shock", "trans")),
        P(None, ("shock", "trans")),
        P(("shock", "trans")),
        P(None, None, ("shock", "trans")),
    )
    return jax.shard_map(shards, mesh=mesh, in_specs=in_specs, out_specs=out_specs, check_vma=False)
```

profile of v0, /device:TPU:99, one launch (start us, length us, event | category | flops | bytes accessed | tf_op | source)
XLA Modules:
  0.0 175.2 jit_solution(1892811446369008532)
XLA Ops:
  0.6 0.8 fusion.49
  1.4 0.7 broadcast_multiply_fusion.3
  2.2 0.8 copy.267
  3.1 0.8 copy.265
  3.9 0.8 constant_dynamic-update-slice_fusion.4
  5.3 1.4 collective-permute-start
  7.2 3.9 %collective-permute-start.1 = (f32[3,32]{0,1:T(8,128)S(1)}, f32[3,32]{0,1:T(8,128)S(1)}, u32[]{:S(2)}, u32[]{:S(2)}) collective-permute-start(f32[3,32]{0,1:T(8,128)S(1)} %bitcast.147), channel_id=1, source_target_pairs={{1,0},{2,1},{3,2},{4,3},{5,4},{6,5},{7,6},{0,7},{9,8},{10,9},{11,1... | collective-permute-start | bytes 1160 | tf_op jit(solution)/shard_map/ppermute | solution.py:22
  13.0 0.8 fusion.51
  14.4 0.8 compare_select_fusion.1
  15.8 0.8 fusion.45
  16.6 0.7 fusion.28
  18.6 1.2 scatter_custom_fusion
  21.7 3.1 %collective-permute-start.3 = (f32[3,128]{0,1:T(8,128)S(1)}, f32[3,128]{0,1:T(8,128)S(1)}, u32[]{:S(2)}, u32[]{:S(2)}) collective-permute-start(f32[3,128]{0,1:T(8,128)S(1)} %bitcast.148), channel_id=1, source_target_pairs={{8,0},{16,8},{24,16},{32,24},{40,32},{48,40},{56,48},{64,56},{72,6... | collective-permute-start | bytes 4616 | tf_op jit(solution)/shard_map/ppermute | solution.py:28
  24.9 4.6 %collective-permute-start.2 = (f32[3,128]{0,1:T(8,128)S(1)}, f32[3,128]{0,1:T(8,128)S(1)}, u32[]{:S(2)}, u32[]{:S(2)}) collective-permute-start(f32[3,128]{0,1:T(8,128)S(1)} %bitcast.149), channel_id=1, source_target_pairs={{0,8},{8,16},{16,24},{24,32},{32,40},{40,48},{48,56},{56,64},{64,7... | collective-permute-start | bytes 4616 | tf_op jit(solution)/shard_map/ppermute | solution.py:28
  32.1 13.1 %gather_fusion.4 = f32[6656,3]{1,0:T(8,128)S(1)} fusion(f32[3,576]{0,1:T(8,128)} %constant_dynamic-update-slice_fusion, s32[7168]{0:T(1024)} %pad_clamp_fusion), kind=kCustom, calls=%fused_computation.4 | custom fusion | bytes 186368 | tf_op jit(solution)/shard_map/while/body/eval_jaxpr/gather | solution.py:120
  45.2 1.3 copy.269
  46.4 0.9 multiply_reduce_fusion.1
  47.3 0.7 multiply_bitcast_fusion.3
  48.1 0.8 broadcast_divide_fusion
  49.7 1.5 stack.123
  51.2 4.5 %copy.271 = f32[35,26,256]{0,1,2:T(8,128)} copy(f32[35,26,256]{2,0,1:T(8,128)S(1)} %stack.123) | data formatting | bytes 1863680 | tf_op jit(solution)/shard_map/while/body/eval_jaxpr/jvp()/stack | solution.py:91
  55.7 5.6 %fusion = f32[4,35,256]{1,0,2:T(4,128)S(1)} fusion(f32[35,26,256]{0,1,2:T(8,128)} %copy.271, f32[4,26,256]{1,0,2:T(4,128)S(1)} %copy.272), kind=kOutput, calls=%fused_computation.15 | convolution fusion | flops 11217920 | bytes 1181696 | tf_op jit(solution)/shard_map/while/body/eval_jaxpr/jvp(nkb,mkb->nmb)/dot_general | solution.py:97
  63.1 1.3 fusion.18
  64.4 2.3 %copy.293 = f32[10,256,35]{2,0,1:T(8,128)S(1)} copy(f32[10,256,35]{1,2,0:T(8,128)} %fusion.18) | data formatting | bytes 716800 | tf_op jit(solution)/shard_map/while/body/eval_jaxpr/transpose(jvp(lm,pmb->plb))/dot_general | solution.py:102
  66.7 0.9 slice_multiply_fusion.15
  67.6 1.1 slice_multiply_fusion.3
  68.8 2.4 %fusion.13 = f32[256,35,4]{1,2,0:T(4,128)S(1)} fusion(f32[1,35,256]{1,0,2:T(1,128)S(1)} %get-tuple-element.114, f32[1,35,256]{1,0,2:T(1,128)S(1)} %get-tuple-element.113, f32[1,35,256]{1,0,2:T(1,128)S(1)} %get-tuple-element.115, f32[1,35,256]{1,0,2:T(1,128)S(1)} %get-tuple-element.112, f32[1,35,256]{1,0,2:T(1,128)S(1)} %get-tuple-element.117, ...), kind=kLoop, calls=%fused_computation.34 | loop fusion | flops 716800 | bytes 716800 | tf_op jit(solution)/shard_map/while/body/eval_jaxpr/transpose(jvp(nkb,mkb->nmb))/transpose | solution.py:97
  71.2 6.8 %fusion.77 = f32[256,4,26]{2,1,0:T(4,128)S(1)} fusion(f32[256,35,4]{1,2,0:T(4,128)S(1)} %fusion.13, f32[35,26,256]{0,1,2:T(8,128)S(1)} %copy-done.1), kind=kOutput, calls=%fused_computation.215 | convolution fusion | flops 11182080 | bytes 1181696 | tf_op jit(solution)/shard_map/while/body/eval_jaxpr/transpose(jvp(nkb,mkb->nmb))/dot_general | solution.py:97
  78.1 8.3 %fusion.76 = f32[256,35,26]{1,2,0:T(8,128)} fusion(f32[256,35,4]{1,2,0:T(4,128)S(1)} %fusion.13, f32[4,26,256]{1,0,2:T(4,128)S(1)} %copy.272), kind=kOutput, calls=%fused_computation.214 | convolution fusion | flops 11182080 | bytes 1181696 | tf_op jit(solution)/shard_map/while/body/eval_jaxpr/transpose(jvp(nkb,mkb->nmb))/dot_general | solution.py:97
  86.4 3.4 %copy.295 = f32[256,35,26]{0,1,2:T(8,128)S(1)} copy(f32[256,35,26]{1,2,0:T(8,128)} %fusion.76) | data formatting | bytes 1863680 | tf_op jit(solution)/shard_map/while/body/eval_jaxpr/transpose(jvp(nkb,mkb->nmb))/dot_general | solution.py:97
  92.6 0.8 fusion.66
  93.4 0.8 copy.299
  94.2 1.9 %copy.298 = f32[6656,3]{1,0:T(8,128)S(1)} copy(f32[6656,3]{0,1:T(4,128)} %bitcast.137) | data formatting | bytes 159744 | tf_op jit(solution)/shard_map/reshape;reshape;transpose | solution.py:136
  96.1 42.0 %scatter_custom_fusion.1 = f32[3,576]{0,1:T(8,128)} fusion(s32[6656]{0:T(1024)} %fusion.28, f32[6656,3]{1,0:T(8,128)S(1)} %copy.298, f32[]{:T(128)} %constant.124.clone.1), kind=kCustom, calls=%fused_computation.39 | custom fusion | flops 19968 | bytes 7424 | tf_op jit(solution)/shard_map/scatter-add | solution.py:136
  138.1 2.3 %fusion.16 = f32[3,576]{0,1:T(8,128)} fusion(f32[3,576]{0,1:T(8,128)} %scatter_custom_fusion.1, f32[3,256]{0,1:T(8,128)} %copy.299, pred[]{:T(512)} %compare_reduce_fusion), kind=kLoop, calls=%fused_computation.41 | loop fusion | flops 2304 | bytes 393728 | tf_op jit(solution)/shard_map/scatter-add | solution.py:137
  140.4 0.9 fusion.74
  141.2 1.9 %collective-permute-start.5 = (f32[3,128]{0,1:T(8,128)S(1)}, f32[3,128]{0,1:T(8,128)S(1)}, u32[]{:S(2)}, u32[]{:S(2)}) collective-permute-start(f32[3,128]{0,1:T(8,128)S(1)} %get-tuple-element.132), channel_id=1, source_target_pairs={{8,0},{16,8},{24,16},{32,24},{40,32},{48,40},{56,48},{64,56},{72,6... | collective-permute-start | bytes 4616 | tf_op jit(solution)/shard_map/ppermute | solution.py:28
  143.2 5.8 %collective-permute-start.4 = (f32[3,128]{0,1:T(8,128)S(1)}, f32[3,128]{0,1:T(8,128)S(1)}, u32[]{:S(2)}, u32[]{:S(2)}) collective-permute-start(f32[3,128]{0,1:T(8,128)S(1)} %get-tuple-element.133), channel_id=1, source_target_pairs={{0,8},{8,16},{16,24},{24,32},{32,40},{40,48},{48,56},{56,64},{64,7... | collective-permute-start | bytes 4616 | tf_op jit(solution)/shard_map/ppermute | solution.py:28
  149.1 0.9 slice.153
  150.3 1.4 scatter_custom_fusion.2
  151.7 1.5 scatter_custom_fusion.3
  153.2 0.9 collective-permute-start.7
  155.3 5.0 %collective-permute-done.6 = f32[3,32]{0,1:T(8,128)S(1)} collective-permute-done((f32[3,32]{0,1:T(8,128)S(1)}, f32[3,32]{0,1:T(8,128)S(1)}, u32[]{:S(2)}, u32[]{:S(2)}) %collective-permute-start.6) | collective-permute-done | bytes 416 | tf_op jit(solution)/shard_map/ppermute | solution.py:22
  160.4 0.9 scatter_custom_fusion.4
  161.3 0.9 scatter_custom_fusion.5
  162.2 1.1 broadcast_multiply_fusion.1
  164.9 1.9 %collective-permute-start.8 = (f32[3,3,16]{2,1,0:T(4,128)S(1)}, f32[3,3,16]{2,1,0:T(4,128)S(1)}, u32[]{:S(2)}, u32[]{:S(2)}) collective-permute-start(f32[3,3,16]{2,1,0:T(4,128)S(1)} %maximum_multiply_fusion), channel_id=1, source_target_pairs={{8,0},{16,8},{24,16},{32,24},{40,32},{48,40},{56,48},{64,56},{72,6... | collective-permute-start | bytes 1736 | tf_op jit(solution)/shard_map/ppermute | solution.py:28
  168.8 5.8 %collective-permute-done.8 = f32[3,3,16]{2,1,0:T(4,128)S(1)} collective-permute-done((f32[3,3,16]{2,1,0:T(4,128)S(1)}, f32[3,3,16]{2,1,0:T(4,128)S(1)}, u32[]{:S(2)}, u32[]{:S(2)}) %collective-permute-start.8) | collective-permute-done | bytes 608 | tf_op jit(solution)/shard_map/ppermute | solution.py:28
  (112 shorter events, 19.8 us)
Async XLA Ops:
  0.6 62.0 %copy-start = (f32[50,50]{1,0:T(8,128)S(1)}, f32[50,50]{1,0:T(8,128)}, u32[]{:S(2)}) copy-start(f32[50,50]{1,0:T(8,128)} %param.20) | copy-start | bytes 30004
  1.4 2.5 %copy-start.12 = (s32[32]{0:T(128)}, s32[32]{0:T(128)S(1)}, u32[]{:S(2)}) copy-start(s32[32]{0:T(128)S(1)} %get-tuple-element.177) | copy-start | bytes 388
  1.4 2.5 %copy-start.13 = (s32[32]{0:T(128)}, s32[32]{0:T(128)S(1)}, u32[]{:S(2)}) copy-start(s32[32]{0:T(128)S(1)} %get-tuple-element.176) | copy-start | bytes 388
  4.7 26.8 %copy-start.2 = (f32[3,256]{0,1:T(8,128)}, f32[3,256]{0,1:T(8,128)S(1)}, u32[]{:S(2)}) copy-start(f32[3,256]{0,1:T(8,128)S(1)} %get-tuple-element.105) | copy-start | bytes 9220
  5.3 15.1 %collective-permute-start = (f32[3,32]{0,1:T(8,128)S(1)}, f32[3,32]{0,1:T(8,128)S(1)}, u32[]{:S(2)}, u32[]{:S(2)}) collective-permute-start(f32[3,32]{0,1:T(8,128)S(1)} %bitcast.146), channel_id=1, source_target_pairs={{7,0},{0,1},{1,2},{2,3},{3,4},{4,5},{5,6},{6,7},{15,8},{8,9},{9,10... | collective-permute-start | bytes 1160 | tf_op jit(solution)/shard_map/ppermute | solution.py:22
  7.2 13.2 %collective-permute-start.1 = (f32[3,32]{0,1:T(8,128)S(1)}, f32[3,32]{0,1:T(8,128)S(1)}, u32[]{:S(2)}, u32[]{:S(2)}) collective-permute-start(f32[3,32]{0,1:T(8,128)S(1)} %bitcast.147), channel_id=1, source_target_pairs={{1,0},{2,1},{3,2},{4,3},{5,4},{6,5},{7,6},{0,7},{9,8},{10,9},{11,1... | collective-permute-start | bytes 1160 | tf_op jit(solution)/shard_map/ppermute | solution.py:22
  13.7 6.7 %copy-start.14 = (s32[128]{0:T(128)}, s32[128]{0:T(128)S(1)}, u32[]{:S(2)}) copy-start(s32[128]{0:T(128)S(1)} %get-tuple-element.175) | copy-start | bytes 1540
  13.7 6.7 %copy-start.15 = (s32[128]{0:T(128)}, s32[128]{0:T(128)S(1)}, u32[]{:S(2)}) copy-start(s32[128]{0:T(128)S(1)} %get-tuple-element.174) | copy-start | bytes 1540
  14.4 6.0 %copy-start.9 = (s32[1024]{0:T(1024)}, s32[1024]{0:T(1024)S(1)}, u32[]{:S(2)}) copy-start(s32[1024]{0:T(1024)S(1)} %pad_clamp_fusion.1) | copy-start | bytes 12292
  21.7 9.7 %collective-permute-start.3 = (f32[3,128]{0,1:T(8,128)S(1)}, f32[3,128]{0,1:T(8,128)S(1)}, u32[]{:S(2)}, u32[]{:S(2)}) collective-permute-start(f32[3,128]{0,1:T(8,128)S(1)} %bitcast.148), channel_id=1, source_target_pairs={{8,0},{16,8},{24,16},{32,24},{40,32},{48,40},{56,48},{64,56},{72,6... | collective-permute-start | bytes 4616 | tf_op jit(solution)/shard_map/ppermute | solution.py:28
  24.9 5.9 %collective-permute-start.2 = (f32[3,128]{0,1:T(8,128)S(1)}, f32[3,128]{0,1:T(8,128)S(1)}, u32[]{:S(2)}, u32[]{:S(2)}) collective-permute-start(f32[3,128]{0,1:T(8,128)S(1)} %bitcast.149), channel_id=1, source_target_pairs={{0,8},{8,16},{16,24},{24,32},{32,40},{40,48},{48,56},{56,64},{64,7... | collective-permute-start | bytes 4616 | tf_op jit(solution)/shard_map/ppermute | solution.py:28
  47.3 0.8 copy-start.3
  55.7 6.5 %copy-start.7 = (f32[5,35,1]{1,0,2:T(8,128)S(1)}, f32[5,35,1]{1,0,2:T(8,128)}, u32[]{:S(2)}) copy-start(f32[5,35,1]{1,0,2:T(8,128)} %constant.203) | copy-start | bytes 2104
  55.7 7.1 %copy-start.11 = (f32[50]{0:T(128)S(1)}, f32[50]{0:T(128)}, u32[]{:S(2)}) copy-start(f32[50]{0:T(128)} %param.19) | copy-start | bytes 604
  66.7 4.5 %copy-start.1 = (f32[35,26,256]{0,1,2:T(8,128)S(1)}, f32[35,26,256]{0,1,2:T(8,128)}, u32[]{:S(2)}) copy-start(f32[35,26,256]{0,1,2:T(8,128)} %copy.271) | copy-start | bytes 2795524
  86.3 5.7 %copy-start.5 = (f32[3,26]{0,1:T(8,128)S(1)}, f32[3,26]{0,1:T(8,128)}, u32[]{:S(2)}) copy-start(f32[3,26]{0,1:T(8,128)} %constant.140.clone) | copy-start | bytes 940
  86.4 5.7 %copy-start.6 = (f32[26,256]{1,0:T(8,128)S(1)}, f32[26,256]{1,0:T(8,128)}, u32[]{:S(2)}) copy-start(f32[26,256]{1,0:T(8,128)} %get-tuple-element.171) | copy-start | bytes 79876
  86.4 6.0 %copy-start.4 = (f32[26,256]{1,0:T(8,128)S(1)}, f32[26,256]{1,0:T(8,128)}, u32[]{:S(2)}) copy-start(f32[26,256]{1,0:T(8,128)} %copy-done.3) | copy-start | bytes 79876
  92.0 62.8 %copy-start.10 = (f32[257]{0:T(512)S(1)}, f32[257]{0:T(512)}, u32[]{:S(2)}) copy-start(f32[257]{0:T(512)} %scatter_custom_fusion) | copy-start | bytes 3088
  94.2 70.7 %copy-start.8 = (f32[3,16]{1,0:T(4,128)S(1)}, f32[3,16]{1,0:T(4,128)}, u32[]{:S(2)}) copy-start(f32[3,16]{1,0:T(4,128)} %copy.300) | copy-start | bytes 580
  94.2 70.7 %copy-start.16 = (f32[16]{0:T(128)S(1)}, f32[16]{0:T(128)}, u32[]{:S(2)}) copy-start(f32[16]{0:T(128)} %compare_convert_fusion) | copy-start | bytes 196
  141.2 10.5 %collective-permute-start.5 = (f32[3,128]{0,1:T(8,128)S(1)}, f32[3,128]{0,1:T(8,128)S(1)}, u32[]{:S(2)}, u32[]{:S(2)}) collective-permute-start(f32[3,128]{0,1:T(8,128)S(1)} %get-tuple-element.132), channel_id=1, source_target_pairs={{8,0},{16,8},{24,16},{32,24},{40,32},{48,40},{56,48},{64,56},{72,6... | collective-permute-start | bytes 4616 | tf_op jit(solution)/shard_map/ppermute | solution.py:28
  143.2 7.1 %collective-permute-start.4 = (f32[3,128]{0,1:T(8,128)S(1)}, f32[3,128]{0,1:T(8,128)S(1)}, u32[]{:S(2)}, u32[]{:S(2)}) collective-permute-start(f32[3,128]{0,1:T(8,128)S(1)} %get-tuple-element.133), channel_id=1, source_target_pairs={{0,8},{8,16},{16,24},{24,32},{32,40},{40,48},{48,56},{56,64},{64,7... | collective-permute-start | bytes 4616 | tf_op jit(solution)/shard_map/ppermute | solution.py:28
  153.2 8.1 %collective-permute-start.7 = (f32[3,32]{0,1:T(8,128)S(1)}, f32[3,32]{0,1:T(8,128)S(1)}, u32[]{:S(2)}, u32[]{:S(2)}) collective-permute-start(f32[3,32]{0,1:T(8,128)S(1)} %get-tuple-element.134), channel_id=1, source_target_pairs={{1,0},{2,1},{3,2},{4,3},{5,4},{6,5},{7,6},{0,7},{9,8},{10,9},{11,1... | collective-permute-start | bytes 1160 | tf_op jit(solution)/shard_map/ppermute | solution.py:22
  154.2 6.2 %collective-permute-start.6 = (f32[3,32]{0,1:T(8,128)S(1)}, f32[3,32]{0,1:T(8,128)S(1)}, u32[]{:S(2)}, u32[]{:S(2)}) collective-permute-start(f32[3,32]{0,1:T(8,128)S(1)} %get-tuple-element.135), channel_id=1, source_target_pairs={{7,0},{0,1},{1,2},{2,3},{3,4},{4,5},{5,6},{6,7},{15,8},{8,9},{9,10... | collective-permute-start | bytes 1160 | tf_op jit(solution)/shard_map/ppermute | solution.py:22
  164.9 9.7 %collective-permute-start.8 = (f32[3,3,16]{2,1,0:T(4,128)S(1)}, f32[3,3,16]{2,1,0:T(4,128)S(1)}, u32[]{:S(2)}, u32[]{:S(2)}) collective-permute-start(f32[3,3,16]{2,1,0:T(4,128)S(1)} %maximum_multiply_fusion), channel_id=1, source_target_pairs={{8,0},{16,8},{24,16},{32,24},{40,32},{48,40},{56,48},{64,56},{72,6... | collective-permute-start | bytes 1736 | tf_op jit(solution)/shard_map/ppermute | solution.py:28
where the time goes:
time: 175 us
  other arithmetic  69.2 us (40%)
  local copies, waits for them, and re-layouts  45.2 us (26%)
  starting transfers between devices  24.1 us (14%)
  matrix products  22.9 us (13%)
  waiting for transfers between devices  11.1 us (6%)
  between operations  2.57 us (1%)
    scatter-add x1, other arithmetic, store_terms(): total = total.at[:, clamped.reshape(-1)].add(pair_grad.reshape(3, -1))  42 us
    dot_general x3, matrix products, block_energy(): jnp.einsum('nkb,mkb->nmb', radial, monomials, precision=highest)  20.7 us
    ppermute x5, starting transfers between devices, passed_along(): return lax.ppermute(x, axis, pairs)  17.4 us
    gather x2, local copies, waits for them, and re-layouts, one_group(): extended[:, clamped_rows]  14.4 us
    ppermute x4, starting transfers between devices, from_behind(): return lax.ppermute(block, axis, route)  6.77 us
    unnamed x44, local copies, waits for them, and re-layouts  6.17 us
    ppermute x5, waiting for transfers between devices, passed_along(): return lax.ppermute(x, axis, pairs)  6.12 us
    another operation x2, local copies, waits for them, and re-layouts, block_energy(): jnp.stack([powers_first[first_power] * powers_second[second_power] * powe...  6.01 us
  transfers between devices with their start and end apart: 9, of which 4 were waited for; matrix products, arithmetic and copies ran while one was open for 9% of the time, Pallas kernels for 0%

commit v1 on v0

v1 whole, which is shorter than its diff:
```python
import functools
import math

import jax
import jax.numpy as jnp
import numpy as np
from jax import lax
from jax.experimental import pallas as pl
from jax.experimental.pallas import tpu as pltpu
from jax.sharding import PartitionSpec as P

F32 = jnp.float32
BF16 = jnp.bfloat16
MESH = pl.DeviceIdType.MESH

kick_factor = 0.5
drift_step = 0.02
cutoff_radius = 4.2
radial_width = 0.35
radial_centers = (1.4, 1.9, 2.4, 2.9)
moment_scale = 0.25
pair_list = ((0, 0), (0, 1), (0, 2), (0, 3), (1, 1), (1, 2), (1, 3), (2, 2), (2, 3), (3, 3))
LANES = 128
ROWS = 32
MROWS = 40
DROWS = 64


def exponents():
    triples = []
    for degree in range(5):
        for p in range(degree, -1, -1):
            for q in range(degree - p, -1, -1):
                triples.append((p, q, degree - p - q))
    return triples


TRIPLES = exponents()
INDEX = {t: i for i, t in enumerate(TRIPLES)}


def lattice_rows():
    entries = []
    for number in range(8):
        entries.append(
            [1.0 - 2.0 * (number >> 2 & 1), 1.0 - 2.0 * (number >> 1 & 1), 1.0 - 2.0 * (number & 1)]
        )
    for axis_pick in range(3):
        for signed in (2.0, -2.0):
            vector = [0.0, 0.0, 0.0]
            vector[axis_pick] = signed
            entries.append(vector)
    for zero_pick in (2, 1, 0):
        others = [axis_pick for axis_pick in range(3) if axis_pick != zero_pick]
        for leading in (2.0, -2.0):
            for trailing in (2.0, -2.0):
                vector = [0.0, 0.0, 0.0]
                vector[others[0]] = leading
                vector[others[1]] = trailing
                entries.append(vector)
    while len(entries) < ROWS:
        entries.append([1.0, 1.0, 1.0])
    table = np.array(entries, dtype=np.float32).T
    return np.broadcast_to(table[:, :, None], (3, ROWS, LANES)).copy()


def contraction_table():
    table = np.zeros((DROWS, len(pair_list) * MROWS), dtype=np.float32)
    for i in range(len(pair_list)):
        for m, (p, q, w) in enumerate(TRIPLES):
            degree = p + q + w
            table[5 * i + degree, MROWS * i + m] = math.factorial(degree) / (
                math.factorial(p) * math.factorial(q) * math.factorial(w)
            )
    return table


def split(x):
    hi = x.astype(BF16)
    lo = (x - hi.astype(F32)).astype(BF16)
    return hi, lo


def mm(a, b):
    return lax.dot_general(a, b, (((1,), (0,)), ((), ())), preferred_element_type=F32)


def mm_nt(a, b):
    return lax.dot_general(a, b, (((1,), (1,)), ((), ())), preferred_element_type=F32)


def lane_gather(x, index):
    numbers = lax.GatherDimensionNumbers(
        offset_dims=(),
        collapsed_slice_dims=(1,),
        start_index_map=(1,),
        operand_batching_dims=(0,),
        start_indices_batching_dims=(0,),
    )
    return lax.gather(
        x,
        index[:, :, None],
        numbers,
        slice_sizes=(1, 1),
        mode=lax.GatherScatterMode.PROMISE_IN_BOUNDS,
    )


def rows_of(row, count):
    return jnp.broadcast_to(row, (count, row.shape[1]))


def sin_of(u):
    s = u * u
    r = -1.0 / 39916800.0
    for c in (1.0 / 362880.0, -1.0 / 5040.0, 1.0 / 120.0, -1.0 / 6.0, 1.0):
        r = r * s + c
    return r * u


def cos_of(u):
    s = u * u
    r = 1.0 / 479001600.0
    for c in (-1.0 / 3628800.0, 1.0 / 40320.0, -1.0 / 720.0, 1.0 / 24.0, -0.5, 1.0):
        r = r * s + c
    return r


def kernel(
    n_shock,
    n_trans,
    disp,
    vel,
    force,
    beta,
    alpha,
    live,
    trans_idx,
    shock_idx,
    nb_block,
    nb_lane,
    leave_idx,
    leave_count,
    offs,
    wmat,
    wmat_t,
    out_disp,
    out_vel,
    out_force,
    out_energy,
    out_arr,
    t_send,
    t_recv,
    s_send,
    s_recv,
    r_send,
    r_recv,
    u_send,
    u_recv,
    v_send,
    v_recv,
    send_sems,
    recv_sems,
    ext,
    blk,
    lan,
    idx_pad,
    geom,
    monos,
    mom,
    dmom,
    onehot,
    grows,
    apad,
    shock_hot,
    trans_hot,
    grads,
    own_sum,
):
    s_me = lax.axis_index("shock")
    t_me = lax.axis_index("trans")
    s_up = lax.rem(s_me + 1, n_shock)
    s_down = lax.rem(s_me + n_shock - 1, n_shock)
    t_up = lax.rem(t_me + 1, n_trans)
    t_down = lax.rem(t_me + n_trans - 1, n_trans)
    near = {
        "t_up": (s_me, t_up),
        "t_down": (s_me, t_down),
        "s_up": (s_up, t_me),
        "s_down": (s_down, t_me),
    }
    barrier = pltpu.get_barrier_semaphore()
    for where in near.values():
        pl.semaphore_signal(barrier, inc=1, device_id=where, device_id_type=MESH)

    def remote(src, dst, k, where):
        return pltpu.make_async_remote_copy(
            src_ref=src,
            dst_ref=dst,
            send_sem=send_sems.at[k],
            recv_sem=recv_sems.at[k],
            device_id=near[where],
            device_id_type=MESH,
        )

    t_copies = (
        remote(t_send, t_recv.at[0], 0, "t_up"),
        remote(t_send, t_recv.at[1], 1, "t_down"),
    )
    s_copies = (
        remote(s_send, s_recv.at[0], 2, "s_up"),
        remote(s_send, s_recv.at[1], 3, "s_down"),
    )
    r_copies = (
        remote(r_send, r_recv.at[0], 4, "s_up"),
        remote(r_send, r_recv.at[1], 5, "s_down"),
    )
    u_copies = (
        remote(u_send, u_recv.at[0], 6, "t_up"),
        remote(u_send, u_recv.at[1], 7, "t_down"),
    )
    v_copy = remote(v_send, v_recv, 8, "s_down")

    lane_row = lax.broadcasted_iota(jnp.int32, (1, LANES), 1)
    lane8 = lax.broadcasted_iota(jnp.int32, (8, LANES), 1)
    sub8 = lax.broadcasted_iota(jnp.int32, (8, LANES), 0)

    half_velocity = vel[...] + kick_factor * force[...]
    displaced = disp[...] + drift_step * half_velocity
    ext[...] = jnp.zeros_like(ext)
    for h in range(2):
        ext[h, 0:3, :] = displaced[:, h * LANES : (h + 1) * LANES]

    idx_pad[...] = jnp.zeros_like(idx_pad)
    idx_pad[0:1, 0:32] = trans_idx[1:2, :]
    idx_pad[1:2, 0:32] = trans_idx[0:1, :]
    idx_pad[2:4, :] = shock_idx[...]
    idx_pad[4:5, 0:16] = leave_idx[...]
    t_row = jnp.where(lane_row < 32, idx_pad[0:1, :], pltpu.roll(idx_pad[1:2, :], 32, 1))
    t_send[...] = lane_gather(ext[0], rows_of(t_row, 8))

    pl.semaphore_wait(barrier, 4)
    for copy in t_copies:
        copy.start()

    shock8 = jnp.where(sub8 < 4, rows_of(idx_pad[2:3, :], 8), rows_of(idx_pad[3:4, :], 8))
    shock_block = shock8 >> 7
    shock_lane = shock8 & 127
    doubled = [jnp.where(sub8 < 4, ext[b], pltpu.roll(ext[b], 4, 0)) for b in range(2)]
    s_own = jnp.where(
        shock_block == 0,
        lane_gather(doubled[0], shock_lane),
        lane_gather(doubled[1], shock_lane),
    )

    blk[...] = jnp.full_like(blk, -1)
    lan[...] = jnp.zeros_like(lan)
    blk[0:26, :] = nb_block[...]
    lan[0:26, :] = nb_lane[...] & 127

    for copy in t_copies:
        copy.wait_recv()
    t_ghost = jnp.where(lane8 < 32, t_recv[0], jnp.where(lane8 < 64, t_recv[1], 0.0))
    t_double = jnp.where(sub8 < 4, t_ghost, pltpu.roll(t_ghost, 4, 0))
    s_send[...] = jnp.where(shock_block == 2, lane_gather(t_double, shock_lane), s_own)
    for copy in s_copies:
        copy.start()

    column = lax.broadcasted_iota(jnp.int32, (LANES, 2 * LANES), 0)

    def fill_onehot(k, carry):
        row = lan[pl.ds(k, 1), :]
        hot = jnp.where(column == rows_of(row, LANES), 1.0, 0.0).astype(BF16)
        onehot[:, pl.ds(pl.multiple_of(k * 2 * LANES, 2 * LANES), 2 * LANES)] = hot
        return carry

    lax.fori_loop(0, 26, fill_onehot, 0)

    column384 = lax.broadcasted_iota(jnp.int32, (3 * LANES, LANES), 0)
    for d in range(2):
        shock_hot[:, d * LANES : (d + 1) * LANES] = jnp.where(
            column384 == rows_of(idx_pad[2 + d : 3 + d, :], 3 * LANES), 1.0, 0.0
        ).astype(BF16)
    column128 = lax.broadcasted_iota(jnp.int32, (LANES, LANES), 0)
    trans_hot[...] = jnp.where(column128 == rows_of(t_row, LANES), 1.0, 0.0).astype(BF16)
    leave_row = idx_pad[4:5, :]
    sending = jnp.where(lane_row < leave_count[0], 1.0, 0.0)
    leave_hot = jnp.where(column128 == rows_of(leave_row, LANES), 1.0, 0.0).astype(BF16)
    departed = mm_nt(rows_of(sending, 16).astype(BF16), leave_hot)[0:1, :]
    keep0 = jnp.where(lane_row < live[0], 1.0, 0.0) * (1.0 - departed)
    keep1 = jnp.where(lane_row + LANES < live[0], 1.0, 0.0)

    apad[...] = jnp.zeros_like(apad)
    apad[0:50, 0:50] = alpha[...]
    sym = 0.5 * (apad[...] + apad[...].T)
    sym_hi, sym_lo = split(sym[0:DROWS, 0:DROWS])
    apad[0:1, :] = jnp.zeros((1, LANES), F32)
    apad[0:1, 0:50] = beta[...]
    beta_col = rows_of(apad[0:1, :], LANES).T[0:DROWS, :]
    beta_col = jnp.concatenate([beta_col, beta_col], axis=1)
    for n in range(4):
        mom[n * MROWS + 32 : (n + 1) * MROWS, :] = jnp.zeros((8, 2 * LANES), F32)

    for copy in s_copies:
        copy.wait_recv()
    lower = jnp.where(s_me > 0, s_recv[0], 0.0)
    upper = jnp.where(s_me < n_shock - 1, s_recv[1], 0.0)
    both = jnp.where(sub8 < 4, pltpu.roll(lower, 4, 0), pltpu.roll(upper, 4, 0))
    turned = pltpu.roll(both, 64, 1)
    swapped = pltpu.roll(turned, 4, 0)
    ext[2] = jnp.where(lane8 < 64, t_ghost, turned)
    ext[3] = jnp.where(lane8 < 64, turned, swapped)
    ext[4] = swapped

    for h in range(2):
        hs = slice(h * LANES, (h + 1) * LANES)
        block = blk[:, hs]
        lane = lan[:, hs]
        parts = []
        for c in range(3):
            found = jnp.zeros((ROWS, LANES), F32)
            for b in range(5):
                value = lane_gather(rows_of(ext[b, c : c + 1, :], ROWS), lane)
                found = jnp.where(block == b, value, found)
            parts.append(offs[c] + found - rows_of(ext[h, c : c + 1, :], ROWS))
        px, py, pz = parts
        square = px * px + py * py + pz * pz
        inverse = lax.rsqrt(square)
        distance = square * inverse
        ux, uy, uz = px * inverse, py * inverse, pz * inverse
        angle = (0.5 * math.pi) - (0.5 * math.pi / cutoff_radius) * distance
        sine, cosine = sin_of(angle), cos_of(angle)
        scale = jnp.where(block >= 0, moment_scale, 0.0)
        smooth = scale * sine * sine
        slope = scale * (-math.pi / cutoff_radius) * sine * cosine
        radial = []
        for n, center in enumerate(radial_centers):
            z = (distance - center) * (1.0 / radial_width)
            e = jnp.exp(-(z * z))
            r = smooth * e
            radial.append(r)
            geom[n, :, hs] = r
            geom[4 + n, :, hs] = slope * e - (2.0 / radial_width) * z * r
        geom[8, :, hs] = ux
        geom[9, :, hs] = uy
        geom[10, :, hs] = uz
        geom[11, :, hs] = inverse
        values = {}
        for m, (p, q, w) in enumerate(TRIPLES):
            if m == 0:
                value = None
            elif p > 0:
                prior = values[(p - 1, q, w)]
                value = ux if prior is None else prior * ux
            elif q > 0:
                prior = values[(p, q - 1, w)]
                value = uy if prior is None else prior * uy
            else:
                prior = values[(p, q, w - 1)]
                value = uz if prior is None else prior * uz
            values[(p, q, w)] = value
            if value is not None:
                monos[m, :, hs] = value
            for n in range(4):
                term = radial[n] if value is None else radial[n] * value
                mom[n * MROWS + m : n * MROWS + m + 1, hs] = jnp.sum(term, axis=0, keepdims=True)

    moments = [mom[n * MROWS : (n + 1) * MROWS, :] for n in range(4)]
    products = jnp.concatenate([moments[n] * moments[o] for n, o in pair_list], axis=0)
    prod_hi, prod_lo = split(products)
    weights = wmat[...]
    descriptor = mm(weights, prod_hi) + mm(weights, prod_lo)
    desc_hi, desc_lo = split(descriptor)
    quadratic = mm(sym_hi, desc_hi) + mm(sym_lo, desc_hi) + mm(sym_hi, desc_lo)
    energy = jnp.sum(descriptor * (beta_col + 0.5 * quadratic), axis=0, keepdims=True)
    slope_hi, slope_lo = split(beta_col + quadratic)
    weights_t = wmat_t[...]
    dproducts = mm(weights_t, slope_hi) + mm(weights_t, slope_lo)
    for n in range(4):
        total = None
        for i, (a, b) in enumerate(pair_list):
            if n not in (a, b):
                continue
            part = dproducts[i * MROWS : (i + 1) * MROWS, :]
            if a == b:
                part = 2.0 * part * moments[n]
            else:
                part = part * moments[b if n == a else a]
            total = part if total is None else total + part
        dmom[n * MROWS : (n + 1) * MROWS, :] = total

    for h in range(2):
        hs = slice(h * LANES, (h + 1) * LANES)
        radial = [geom[n, :, hs] for n in range(4)]
        dradial = [None] * 4
        sums = {}
        for m, (p, q, w) in enumerate(TRIPLES):
            coefficient = None
            for n in range(4):
                row = rows_of(dmom[n * MROWS + m : n * MROWS + m + 1, hs], ROWS)
                term = row if m == 0 else row * monos[m, :, hs]
                dradial[n] = term if dradial[n] is None else dradial[n] + term
                if m > 0:
                    term = row * radial[n]
                    coefficient = term if coefficient is None else coefficient + term
            if m == 0:
                continue
            for c, (power, prior) in enumerate(
                ((p, (p - 1, q, w)), (q, (p, q - 1, w)), (w, (p, q, w - 1)))
            ):
                if power == 0:
                    continue
                at = INDEX[prior]
                term = coefficient if at == 0 else coefficient * monos[at, :, hs]
                key = (c, power)
                sums[key] = term if key not in sums else sums[key] + term
        unit = [geom[8 + c, :, hs] for c in range(3)]
        inverse = geom[11, :, hs]
        along = None
        for n in range(4):
            term = geom[4 + n, :, hs] * dradial[n]
            along = term if along is None else along + term
        tangent = []
        for c in range(3):
            total = sums[(c, 1)]
            for power in (2, 3, 4):
                total = total + float(power) * sums[(c, power)]
            tangent.append(total * inverse)
        inner = unit[0] * tangent[0] + unit[1] * tangent[1] + unit[2] * tangent[2]
        along = along - inner
        for c in range(3):
            g = tangent[c] + unit[c] * along
            grads[c, :, hs] = g
            own_sum[h, c : c + 1, :] = jnp.sum(g, axis=0, keepdims=True)

    sub24 = lax.broadcasted_iota(jnp.int32, (24, 2 * LANES), 0)
    row_block = sub24 >> 2
    row_part = sub24 & 3

    def fill_rows(k, carry):
        gx = rows_of(grads[0, pl.ds(k, 1), :], 24)
        gy = rows_of(grads[1, pl.ds(k, 1), :], 24)
        gz = rows_of(grads[2, pl.ds(k, 1), :], 24)
        value = jnp.where(row_part == 0, gx, jnp.where(row_part == 1, gy, gz))
        value = jnp.where(row_block == rows_of(blk[pl.ds(k, 1), :], 24), value, 0.0)
        hi = value.astype(BF16).astype(F32)
        at = pl.ds(pl.multiple_of(k * 2 * LANES, 2 * LANES), 2 * LANES)
        grows[:, at] = jnp.concatenate([hi, value - hi], axis=0).astype(BF16)
        return carry

    lax.fori_loop(0, 26, fill_rows, 0)
    spread = mm_nt(grows[...], onehot[...])
    spread = spread[0:24, :] + spread[24:48, :]
    first = spread[0:8, :]
    second = spread[8:16, :]
    third = spread[16:24, :]
    second_turned = pltpu.roll(second, 64, 1)
    third_turned = pltpu.roll(third, 64, 1)
    shifted = jnp.where(
        sub8 < 4, pltpu.roll(second_turned, 4, 0), pltpu.roll(third_turned, 4, 0)
    )
    r_send[...] = jnp.where(lane8 < 64, second_turned, shifted)
    for copy in r_copies:
        copy.start()
    for copy in r_copies:
        copy.wait_recv()

    from_lower = jnp.where(s_me > 0, pltpu.roll(r_recv[0], 4, 0), 0.0)
    from_upper = jnp.where(s_me < n_shock - 1, r_recv[1], 0.0)
    back = jnp.concatenate([from_lower, from_upper], axis=1)
    back_hi = back.astype(BF16).astype(F32)
    back2 = jnp.concatenate([back_hi, back - back_hi], axis=0).astype(BF16)
    added = mm_nt(back2, shock_hot[...])
    added = added[0:8, :] + added[8:16, :]
    u_send[...] = second + added[:, 2 * LANES : 3 * LANES]
    for copy in u_copies:
        copy.start()

    first_swapped = pltpu.roll(first, 4, 0)
    grad0 = first + added[:, 0:LANES] - own_sum[0]
    grad1 = first_swapped + added[:, LANES : 2 * LANES] - own_sum[1]
    force1 = -grad1[0:3, :]
    half1 = half_velocity[:, LANES:]
    out_disp[:, LANES:] = displaced[:, LANES:] * rows_of(keep1, 3)
    out_vel[:, LANES:] = (half1 + kick_factor * force1) * rows_of(keep1, 3)
    out_force[:, LANES:] = force1 * rows_of(keep1, 3)
    out_energy[:, 0:LANES] = energy[:, 0:LANES] * keep0
    out_energy[:, LANES:] = energy[:, LANES:] * keep1
    out_disp[:, 0:LANES] = displaced[:, 0:LANES] * rows_of(keep0, 3)

    for copy in u_copies:
        copy.wait_recv()
    merged = jnp.where(lane8 < 32, u_recv[1], jnp.where(lane8 < 64, u_recv[0], 0.0))
    merged_hi = merged.astype(BF16).astype(F32)
    merged2 = jnp.concatenate([merged_hi, merged - merged_hi], axis=0).astype(BF16)
    added = mm_nt(merged2, trans_hot[...])
    force0 = -(grad0 + added[0:8, :] + added[8:16, :])[0:3, :]
    velocity0 = half_velocity[:, 0:LANES] + kick_factor * force0
    ext[5, 0:3, :] = velocity0
    ext[6, 0:3, :] = force0
    leave3 = rows_of(leave_row, 8)
    for q, at in enumerate((0, 5, 6)):
        v_send[q] = lane_gather(ext[at], leave3) * rows_of(sending, 8)
    v_copy.start()
    out_vel[:, 0:LANES] = velocity0 * rows_of(keep0, 3)
    out_force[:, 0:LANES] = force0 * rows_of(keep0, 3)
    v_copy.wait_recv()
    for q in range(3):
        out_arr[q] = jnp.where(s_me < n_shock - 1, v_recv[q, 0:3, 0:16], 0.0)
    for copy in (*t_copies, *s_copies, *r_copies, *u_copies, v_copy):
        copy.wait_send()


def whole_step(n_shock, n_trans, *args):
    (disp, vel, force, beta, alpha, live, trans_idx, shock_idx, block, lane, leave, count) = args
    table = contraction_table()
    vmem = pl.BlockSpec(memory_space=pltpu.VMEM)
    smem = pl.BlockSpec(memory_space=pltpu.SMEM)
    tile = (8, LANES)
    outs = pl.pallas_call(
        functools.partial(kernel, n_shock, n_trans),
        out_shape=(
            jax.ShapeDtypeStruct((3, 256), F32),
            jax.ShapeDtypeStruct((3, 256), F32),
            jax.ShapeDtypeStruct((3, 256), F32),
            jax.ShapeDtypeStruct((1, 256), F32),
            jax.ShapeDtypeStruct((3, 3, 16), F32),
        ),
        in_specs=[vmem] * 5 + [smem] + [vmem] * 5 + [smem] + [vmem] * 3,
        out_specs=(vmem,) * 5,
        scratch_shapes=[
            pltpu.VMEM(tile, F32),
            pltpu.VMEM((2, *tile), F32),
            pltpu.VMEM(tile, F32),
            pltpu.VMEM((2, *tile), F32),
            pltpu.VMEM(tile, F32),
            pltpu.VMEM((2, *tile), F32),
            pltpu.VMEM(tile, F32),
            pltpu.VMEM((2, *tile), F32),
            pltpu.VMEM((3, *tile), F32),
            pltpu.VMEM((3, *tile), F32),
            pltpu.SemaphoreType.DMA((9,)),
            pltpu.SemaphoreType.DMA((9,)),
            pltpu.VMEM((7, *tile), F32),
            pltpu.VMEM((ROWS, 256), jnp.int32),
            pltpu.VMEM((ROWS, 256), jnp.int32),
            pltpu.VMEM(tile, jnp.int32),
            pltpu.VMEM((12, ROWS, 256), F32),
            pltpu.VMEM((35, ROWS, 256), F32),
            pltpu.VMEM((4 * MROWS, 256), F32),
            pltpu.VMEM((4 * MROWS, 256), F32),
            pltpu.VMEM((LANES, 26 * 256), BF16),
            pltpu.VMEM((48, 26 * 256), BF16),
            pltpu.VMEM((LANES, LANES), F32),
            pltpu.VMEM((3 * LANES, 2 * LANES), BF16),
            pltpu.VMEM((LANES, LANES), BF16),
            pltpu.VMEM((3, ROWS, 256), F32),
            pltpu.VMEM((2, *tile), F32),
        ],
        compiler_params=pltpu.CompilerParams(collective_id=0, has_side_effects=True),
        name="whole_step",
    )(
        disp,
        vel,
        force,
        beta.reshape(1, 50),
        alpha,
        live,
        trans_idx,
        shock_idx,
        block,
        lane,
        leave.reshape(1, 16),
        count,
        jnp.asarray(lattice_rows()),
        jnp.asarray(table, BF16),
        jnp.asarray(table.T, BF16),
    )
    return outs[0], outs[1], outs[2], outs[3].reshape(256), outs[4]


def solution(mesh):
    split_1 = P(None, ("shock", "trans"))
    split_0 = P(("shock", "trans"))
    in_specs = (
        split_1,
        split_1,
        split_1,
        P(),
        P(),
        split_0,
        split_1,
        split_1,
        split_1,
        split_1,
        split_0,
        split_0,
    )
    out_specs = (split_1, split_1, split_1, split_0, P(None, None, ("shock", "trans")))
    body = functools.partial(whole_step, mesh.shape["shock"], mesh.shape["trans"])
    return jax.shard_map(body, mesh=mesh, in_specs=in_specs, out_specs=out_specs, check_vma=False)
```

time: 175 us -> 37.7 us (0.22)
  other arithmetic: 69.2 us -> 0 us
  local copies, waits for them, and re-layouts: 45.2 us -> 3.84 us
  Pallas kernels: 0 us -> 31.7 us
  starting transfers between devices: 24.1 us -> 0 us
  matrix products: 22.9 us -> 0 us
  waiting for transfers between devices: 11.1 us -> 0 us
    scatter-add x6 -> x0, other arithmetic: 49 us -> none  [the longest x1 42 us: store_terms(): total = total.at[:, clamped.reshape(-1)].add(pair_grad.reshape(3, -1))]
    pallas_call x0 -> x1, Pallas kernels: none -> 31.7 us  [whole_step(): pl.pallas_call(functools.partial(kernel, n_shock, n_trans), out_shape=(ja...]
    ppermute x9 -> x0, starting transfers between devices: 24.1 us -> none  [the longest x5 17.4 us: passed_along(): return lax.ppermute(x, axis, pairs)]
    dot_general x8 -> x0, matrix products: 22.9 us -> none  [the longest x3 20.7 us: block_energy(): jnp.einsum('nkb,mkb->nmb', radial, monomials, precision=highest)]
    gather x12 -> x0, local copies, waits for them, and re-layouts: 19.5 us -> none  [the longest x2 14.4 us: one_group(): extended[:, clamped_rows]]
    ppermute x9 -> x0, waiting for transfers between devices: 11.1 us -> none  [the longest x5 6.12 us: passed_along(): return lax.ppermute(x, axis, pairs)]
    another operation x6 -> x0, local copies, waits for them, and re-layouts: 8.19 us -> none  [the longest x2 6.01 us: block_energy(): jnp.stack([powers_first[first_power] * powers_second[second_power] * powe...]
    dot_general x3 -> x0, local copies, waits for them, and re-layouts: 5.95 us -> none  [the longest x2 3.64 us: block_energy(): jnp.einsum('nkb,mkb->nmb', radial, monomials, precision=highest)]
  transfers between devices with their start and end apart: 9 -> 0, of which waited for: 4 -> 0; matrix products, arithmetic and copies ran while one was open for 9% -> 0% of each run, Pallas kernels for 0% -> 0%
where the time goes in v1:
time: 37.7 us; the launch traced here: 37.5 us
  Pallas kernels  31.7 us (84%)
  local copies, waits for them, and re-layouts  3.84 us (10%)
  between operations  1.95 us (5%)
    pallas_call x1, Pallas kernels, whole_step(): pl.pallas_call(functools.partial(kernel, n_shock, n_trans), out_shape=(ja...  31.7 us
    unnamed x15, local copies, waits for them, and re-layouts  3.84 us

profile of v1, /device:TPU:99, one launch (start us, length us, event | category | flops | bytes accessed | tf_op | source)
XLA Modules:
  0.0 37.5 jit_solution(14725946276036041841)
XLA Ops:
  1.9 31.7 %whole_step.1 = (f32[3,256]{1,0:T(4,128)}, f32[3,256]{1,0:T(4,128)}, f32[3,256]{1,0:T(4,128)}, f32[1,256]{1,0:T(1,128)}, f32[3,3,16]{2,1,0:T(4,128)}) custom-call(f32[3,256]{1,0:T(4,128)} %disp.1, f32[3,256]{1,0:T(4,128)} %vel.1, f32[3,256]{1,0:T(4,128)} %force.1, f32[1,50]{1,0:T(1,128)} %bitcast.4, f32[50,50]{1,0:T(8,128)} %alpha.1, s32[1]{0:T(128)S(6)} %copy.25.live, ...), custom_call_target="tpu_custom_call" | custom-call | tf_op jit(solution)/shard_map/whole_step/pallas_call | solution.py:520
  33.6 0.0 copy-start.3
  33.6 0.7 %copy-done.3 = f32[3,256]{1,0:T(4,128)S(1)} copy-done((f32[3,256]{1,0:T(4,128)S(1)}, f32[3,256]{1,0:T(4,128)}, u32[]{:S(2)}) %copy-start.3) | copy-done | bytes 3096
  34.3 0.0 copy-start.2
  34.3 0.6 %copy.27 = f32[3,256]{1,0:T(4,128)} copy(f32[3,256]{1,0:T(4,128)S(1)} %copy-done.3) | data formatting | bytes 6144
  34.9 0.1 copy-done.2
  35.0 0.0 copy-start.1
  35.0 0.6 %copy.28 = f32[3,256]{1,0:T(4,128)} copy(f32[3,256]{1,0:T(4,128)S(1)} %copy-done.2) | data formatting | bytes 6144
  35.6 0.1 copy-done.1
  35.7 0.0 copy-start.4
  35.7 0.0 copy-start
  35.7 0.6 %copy.29 = f32[3,256]{1,0:T(4,128)} copy(f32[3,256]{1,0:T(4,128)S(1)} %copy-done.1) | data formatting | bytes 6144
  36.3 0.1 copy-done.4
  36.3 0.6 %copy.30 = f32[256]{0:T(256)} copy(f32[256]{0:T(256)S(1)} %bitcast.3) | data formatting | bytes 2048
  36.9 0.0 copy-done
  36.9 0.6 %copy.31 = f32[3,3,16]{2,1,0:T(4,128)} copy(f32[3,3,16]{2,1,0:T(4,128)S(1)} %copy-done) | data formatting | bytes 1152
Async XLA Ops:
  33.6 0.7 %copy-start.3 = (f32[3,256]{1,0:T(4,128)S(1)}, f32[3,256]{1,0:T(4,128)}, u32[]{:S(2)}) copy-start(f32[3,256]{1,0:T(4,128)} %get-tuple-element.20) | copy-start | bytes 9220
  34.3 0.7 %copy-start.2 = (f32[3,256]{1,0:T(4,128)S(1)}, f32[3,256]{1,0:T(4,128)}, u32[]{:S(2)}) copy-start(f32[3,256]{1,0:T(4,128)} %get-tuple-element.21) | copy-start | bytes 9220
  35.0 0.7 %copy-start.1 = (f32[3,256]{1,0:T(4,128)S(1)}, f32[3,256]{1,0:T(4,128)}, u32[]{:S(2)}) copy-start(f32[3,256]{1,0:T(4,128)} %get-tuple-element.22) | copy-start | bytes 9220
  35.7 0.7 %copy-start.4 = (f32[1,256]{1,0:T(1,128)S(1)}, f32[1,256]{1,0:T(1,128)}, u32[]{:S(2)}) copy-start(f32[1,256]{1,0:T(1,128)} %get-tuple-element.13) | copy-start | bytes 3076
  35.7 1.2 %copy-start = (f32[3,3,16]{2,1,0:T(4,128)S(1)}, f32[3,3,16]{2,1,0:T(4,128)}, u32[]{:S(2)}) copy-start(f32[3,3,16]{2,1,0:T(4,128)} %get-tuple-element.24) | copy-start | bytes 1732

commit v2 on v1

--- a/solution.py
+++ b/solution.py
@@ -126,146 +126,173 @@
     return r
 
 
-def kernel(
-    n_shock,
-    n_trans,
-    disp,
-    vel,
-    force,
-    beta,
-    alpha,
-    live,
-    trans_idx,
-    shock_idx,
-    nb_block,
-    nb_lane,
-    leave_idx,
-    leave_count,
-    offs,
-    wmat,
-    wmat_t,
-    out_disp,
-    out_vel,
-    out_force,
-    out_energy,
-    out_arr,
-    t_send,
-    t_recv,
-    s_send,
-    s_recv,
-    r_send,
-    r_recv,
-    u_send,
-    u_recv,
-    v_send,
-    v_recv,
-    send_sems,
-    recv_sems,
-    ext,
-    blk,
-    lan,
-    idx_pad,
-    geom,
-    monos,
-    mom,
-    dmom,
-    onehot,
-    grows,
-    apad,
-    shock_hot,
-    trans_hot,
-    grads,
-    own_sum,
-):
+DIRS = ((0, 1), (0, -1), (1, 0), (-1, 0), (1, 1), (1, -1), (-1, 1), (-1, -1))
+N_IN = 15
+
+
+def kernel(n_shock, n_trans, *refs):
+    hbm = refs[:N_IN]
+    out_disp, out_vel, out_force, out_energy, out_arr = refs[N_IN : N_IN + 5]
+    (
+        disp,
+        vel,
+        force,
+        beta,
+        alpha,
+        live,
+        trans_idx,
+        shock_idx,
+        nb_block,
+        nb_lane,
+        leave_idx,
+        leave_count,
+        offs,
+        wmat,
+        wmat_t,
+        in_sems,
+        t_send,
+        s_send,
+        f_recv,
+        u_send,
+        r_send,
+        b_recv,
+        v_send,
+        v_recv,
+        f_send_sems,
+        f_recv_sems,
+        b_send_sems,
+        b_recv_sems,
+        v_sems,
+        ext,
+        blk,
+        lan,
+        idx_pad,
+        near_own,
+        geom,
+        monos,
+        mom,
+        dmom,
+        onehot,
+        apad,
+        hot0,
+        hot1,
+        grads,
+        own_sum,
+    ) = refs[N_IN + 5 :]
+    local = (
+        disp,
+        vel,
+        force,
+        beta,
+        alpha,
+        live,
+        trans_idx,
+        shock_idx,
+        nb_block,
+        nb_lane,
+        leave_idx,
+        leave_count,
+        offs,
+        wmat,
+        wmat_t,
+    )
+    loads = [
+        pltpu.make_async_copy(src, dst, in_sems.at[i])
+        for i, (src, dst) in enumerate(zip(hbm, local, strict=True))
+    ]
+    for i in (0, 1, 2, 6, 7, 8, 9, 10, 5, 11, 4, 3, 12, 13, 14):
+        loads[i].start()
+
     s_me = lax.axis_index("shock")
     t_me = lax.axis_index("trans")
-    s_up = lax.rem(s_me + 1, n_shock)
-    s_down = lax.rem(s_me + n_shock - 1, n_shock)
-    t_up = lax.rem(t_me + 1, n_trans)
-    t_down = lax.rem(t_me + n_trans - 1, n_trans)
-    near = {
-        "t_up": (s_me, t_up),
-        "t_down": (s_me, t_down),
-        "s_up": (s_up, t_me),
-        "s_down": (s_down, t_me),
-    }
+
+    def place(ds, dt):
+        return (
+            lax.rem(s_me + (ds + n_shock), n_shock),
+            lax.rem(t_me + (dt + n_trans), n_trans),
+        )
+
     barrier = pltpu.get_barrier_semaphore()
-    for where in near.values():
-        pl.semaphore_signal(barrier, inc=1, device_id=where, device_id_type=MESH)
-
-    def remote(src, dst, k, where):
+    for ds, dt in DIRS:
+        pl.semaphore_signal(barrier, inc=1, device_id=place(ds, dt), device_id_type=MESH)
+
+    def remote(src, dst, send_sem, recv_sem, where):
         return pltpu.make_async_remote_copy(
             src_ref=src,
             dst_ref=dst,
-            send_sem=send_sems.at[k],
-            recv_sem=recv_sems.at[k],
-            device_id=near[where],
+            send_sem=send_sem,
+            recv_sem=recv_sem,
+            device_id=place(*where),
             device_id_type=MESH,
         )
 
-    t_copies = (
-        remote(t_send, t_recv.at[0], 0, "t_up"),
-        remote(t_send, t_recv.at[1], 1, "t_down"),
-    )
-    s_copies = (
-        remote(s_send, s_recv.at[0], 2, "s_up"),
-        remote(s_send, s_recv.at[1], 3, "s_down"),
-    )
-    r_copies = (
-        remote(r_send, r_recv.at[0], 4, "s_up"),
-        remote(r_send, r_recv.at[1], 5, "s_down"),
-    )
-    u_copies = (
-        remote(u_send, u_recv.at[0], 6, "t_up"),
-        remote(u_send, u_recv.at[1], 7, "t_down"),
-    )
-    v_copy = remote(v_send, v_recv, 8, "s_down")
+    forward = [
+        remote(
+            s_send if dt == 0 else t_send,
+            f_recv.at[k],
+            f_send_sems.at[k],
+            f_recv_sems.at[k],
+            (ds, dt),
+        )
+        for k, (ds, dt) in enumerate(DIRS)
+    ]
+    backward = [
+        remote(
+            u_send if ds == 0 else r_send,
+            b_recv.at[k],
+            b_send_sems.at[k],
+            b_recv_sems.at[k],
+            (ds, dt),
+        )
+        for k, (ds, dt) in enumerate(DIRS)
+    ]
+    v_copy = remote(v_send, v_recv, v_sems.at[0], v_sems.at[1], (-1, 0))
+
+    def slot(ds, dt):
+        return DIRS.index((-ds, -dt))
 
     lane_row = lax.broadcasted_iota(jnp.int32, (1, LANES), 1)
     lane8 = lax.broadcasted_iota(jnp.int32, (8, LANES), 1)
     sub8 = lax.broadcasted_iota(jnp.int32, (8, LANES), 0)
-
+    has_lower = jnp.where(s_me > 0, 1, 0)
+    has_upper = jnp.where(s_me < n_shock - 1, 1, 0)
+
+    idx_pad[...] = jnp.zeros_like(idx_pad)
+    ext[...] = jnp.zeros_like(ext)
+    for i in (0, 1, 2, 6, 7):
+        loads[i].wait()
     half_velocity = vel[...] + kick_factor * force[...]
     displaced = disp[...] + drift_step * half_velocity
-    ext[...] = jnp.zeros_like(ext)
     for h in range(2):
         ext[h, 0:3, :] = displaced[:, h * LANES : (h + 1) * LANES]
-
-    idx_pad[...] = jnp.zeros_like(idx_pad)
     idx_pad[0:1, 0:32] = trans_idx[1:2, :]
     idx_pad[1:2, 0:32] = trans_idx[0:1, :]
     idx_pad[2:4, :] = shock_idx[...]
-    idx_pad[4:5, 0:16] = leave_idx[...]
     t_row = jnp.where(lane_row < 32, idx_pad[0:1, :], pltpu.roll(idx_pad[1:2, :], 32, 1))
-    t_send[...] = lane_gather(ext[0], rows_of(t_row, 8))
-
-    pl.semaphore_wait(barrier, 4)
-    for copy in t_copies:
-        copy.start()
-
     shock8 = jnp.where(sub8 < 4, rows_of(idx_pad[2:3, :], 8), rows_of(idx_pad[3:4, :], 8))
     shock_block = shock8 >> 7
     shock_lane = shock8 & 127
     doubled = [jnp.where(sub8 < 4, ext[b], pltpu.roll(ext[b], 4, 0)) for b in range(2)]
+    t_send[...] = lane_gather(ext[0], rows_of(t_row, 8))
+    t_send[4:6, :] = shock_idx[...].astype(F32)
     s_own = jnp.where(
         shock_block == 0,
         lane_gather(doubled[0], shock_lane),
-        lane_gather(doubled[1], shock_lane),
-    )
-
+        jnp.where(shock_block == 1, lane_gather(doubled[1], shock_lane), 0.0),
+    )
+    s_send[...] = jnp.where((sub8 & 3) == 3, shock8.astype(F32), s_own)
+
+    pl.semaphore_wait(barrier, len(DIRS))
+    for k in (4, 5, 6, 7, 0, 1, 2, 3):
+        forward[k].start()
+
+    for i in (8, 9, 10, 5, 11, 4, 3):
+        loads[i].wait()
     blk[...] = jnp.full_like(blk, -1)
     lan[...] = jnp.zeros_like(lan)
     blk[0:26, :] = nb_block[...]
     lan[0:26, :] = nb_lane[...] & 127
-
-    for copy in t_copies:
-        copy.wait_recv()
-    t_ghost = jnp.where(lane8 < 32, t_recv[0], jnp.where(lane8 < 64, t_recv[1], 0.0))
-    t_double = jnp.where(sub8 < 4, t_ghost, pltpu.roll(t_ghost, 4, 0))
-    s_send[...] = jnp.where(shock_block == 2, lane_gather(t_double, shock_lane), s_own)
-    for copy in s_copies:
-        copy.start()
-
+    idx_pad[4:5, 0:16] = leave_idx[...]
     column = lax.broadcasted_iota(jnp.int32, (LANES, 2 * LANES), 0)
 
     def fill_onehot(k, carry):
@@ -275,20 +302,29 @@
         return carry
 
     lax.fori_loop(0, 26, fill_onehot, 0)
-
-    column384 = lax.broadcasted_iota(jnp.int32, (3 * LANES, LANES), 0)
-    for d in range(2):
-        shock_hot[:, d * LANES : (d + 1) * LANES] = jnp.where(
-            column384 == rows_of(idx_pad[2 + d : 3 + d, :], 3 * LANES), 1.0, 0.0
-        ).astype(BF16)
+    for i in (12, 13, 14):
+        loads[i].wait()
+    for h in range(2):
+        hs = slice(h * LANES, (h + 1) * LANES)
+        for c in range(3):
+            found = offs[c] - rows_of(ext[h, c : c + 1, :], ROWS)
+            parts = [
+                lane_gather(rows_of(ext[b, c : c + 1, :], ROWS), lan[:, hs]) for b in range(2)
+            ]
+            block = blk[:, hs]
+            near_own[c, :, hs] = found + jnp.where(
+                block == 0, parts[0], jnp.where(block == 1, parts[1], 0.0)
+            )
+
     column128 = lax.broadcasted_iota(jnp.int32, (LANES, LANES), 0)
-    trans_hot[...] = jnp.where(column128 == rows_of(t_row, LANES), 1.0, 0.0).astype(BF16)
     leave_row = idx_pad[4:5, :]
     sending = jnp.where(lane_row < leave_count[0], 1.0, 0.0)
     leave_hot = jnp.where(column128 == rows_of(leave_row, LANES), 1.0, 0.0).astype(BF16)
     departed = mm_nt(rows_of(sending, 16).astype(BF16), leave_hot)[0:1, :]
     keep0 = jnp.where(lane_row < live[0], 1.0, 0.0) * (1.0 - departed)
     keep1 = jnp.where(lane_row + LANES < live[0], 1.0, 0.0)
+    out_disp[:, 0:LANES] = displaced[:, 0:LANES] * rows_of(keep0, 3)
+    out_disp[:, LANES:] = displaced[:, LANES:] * rows_of(keep1, 3)
 
     apad[...] = jnp.zeros_like(apad)
     apad[0:50, 0:50] = alpha[...]
@@ -301,11 +337,25 @@
     for n in range(4):
         mom[n * MROWS + 32 : (n + 1) * MROWS, :] = jnp.zeros((8, 2 * LANES), F32)
 
-    for copy in s_copies:
+    for copy in forward:
         copy.wait_recv()
-    lower = jnp.where(s_me > 0, s_recv[0], 0.0)
-    upper = jnp.where(s_me < n_shock - 1, s_recv[1], 0.0)
-    both = jnp.where(sub8 < 4, pltpu.roll(lower, 4, 0), pltpu.roll(upper, 4, 0))
+
+    def between(lower, upper):
+        return jnp.where(lane8 < 32, lower, jnp.where(lane8 < 64, upper, 0.0))
+
+    t_ghost = between(f_recv[slot(0, -1)], f_recv[slot(0, 1)])
+    from_low = f_recv[slot(-1, 0)]
+    from_up = f_recv[slot(1, 0)]
+    lists = jnp.where(sub8 < 4, rows_of(from_low[7:8, :], 8), rows_of(from_up[3:4, :], 8))
+    lists = lists.astype(jnp.int32)
+    across = jnp.where(
+        sub8 < 4,
+        between(f_recv[slot(-1, -1)], f_recv[slot(-1, 1)]),
+        pltpu.roll(between(f_recv[slot(1, -1)], f_recv[slot(1, 1)]), 4, 0),
+    )
+    direct = jnp.where(sub8 < 4, pltpu.roll(from_low, 4, 0), pltpu.roll(from_up, 4, 0))
+    both = jnp.where(lists >= 256, lane_gather(across, lists & 127), direct)
+    both = jnp.where(jnp.where(sub8 < 4, has_lower, has_upper) > 0, both, 0.0)
     turned = pltpu.roll(both, 64, 1)
     swapped = pltpu.roll(turned, 4, 0)
     ext[2] = jnp.where(lane8 < 64, t_ghost, turned)
@@ -319,10 +369,10 @@
         parts = []
         for c in range(3):
             found = jnp.zeros((ROWS, LANES), F32)
-            for b in range(5):
+            for b in range(2, 5):
                 value = lane_gather(rows_of(ext[b, c : c + 1, :], ROWS), lane)
                 found = jnp.where(block == b, value, found)
-            parts.append(offs[c] + found - rows_of(ext[h, c : c + 1, :], ROWS))
+            parts.append(near_own[c, :, hs] + found)
         px, py, pz = parts
         square = px * px + py * py + pz * pz
         inverse = lax.rsqrt(square)
@@ -436,130 +486,113 @@
     sub24 = lax.broadcasted_iota(jnp.int32, (24, 2 * LANES), 0)
     row_block = sub24 >> 2
     row_part = sub24 & 3
-
-    def fill_rows(k, carry):
-        gx = rows_of(grads[0, pl.ds(k, 1), :], 24)
-        gy = rows_of(grads[1, pl.ds(k, 1), :], 24)
-        gz = rows_of(grads[2, pl.ds(k, 1), :], 24)
+    spread = jnp.zeros((48, LANES), F32)
+    for k in range(26):
+        gx = rows_of(grads[0, k : k + 1, :], 24)
+        gy = rows_of(grads[1, k : k + 1, :], 24)
+        gz = rows_of(grads[2, k : k + 1, :], 24)
         value = jnp.where(row_part == 0, gx, jnp.where(row_part == 1, gy, gz))
-        value = jnp.where(row_block == rows_of(blk[pl.ds(k, 1), :], 24), value, 0.0)
+        value = jnp.where(row_block == rows_of(blk[k : k + 1, :], 24), value, 0.0)
         hi = value.astype(BF16).astype(F32)
-        at = pl.ds(pl.multiple_of(k * 2 * LANES, 2 * LANES), 2 * LANES)
-        grows[:, at] = jnp.concatenate([hi, value - hi], axis=0).astype(BF16)
-        return carry
-
-    lax.fori_loop(0, 26, fill_rows, 0)
-    spread = mm_nt(grows[...], onehot[...])
+        pieces = jnp.concatenate([hi, value - hi], axis=0).astype(BF16)
+        spread = spread + mm_nt(pieces, onehot[:, k * 2 * LANES : (k + 1) * 2 * LANES])
     spread = spread[0:24, :] + spread[24:48, :]
     first = spread[0:8, :]
     second = spread[8:16, :]
     third = spread[16:24, :]
+    u_send[...] = second
     second_turned = pltpu.roll(second, 64, 1)
     third_turned = pltpu.roll(third, 64, 1)
     shifted = jnp.where(
         sub8 < 4, pltpu.roll(second_turned, 4, 0), pltpu.roll(third_turned, 4, 0)
     )
     r_send[...] = jnp.where(lane8 < 64, second_turned, shifted)
-    for copy in r_copies:
-        copy.start()
-    for copy in r_copies:
+    for k in (4, 5, 6, 7, 0, 1, 2, 3):
+        backward[k].start()
+
+    t_row8 = rows_of(t_row, 8)
+    up_tile = f_recv[slot(0, 1)]
+    down_tile = f_recv[slot(0, -1)]
+    table = jnp.where(sub8 < 4, pltpu.roll(up_tile, 6, 0), down_tile).astype(jnp.int32)
+    through = lane_gather(t_row8, table & 127)
+    start = jnp.where(sub8 < 4, 256, 288)
+    through = jnp.where(table >= start, jnp.where(table < start + 32, through, -1), -1)
+    direct = idx_pad[2:4, :]
+    direct = jnp.where(direct < 256, direct, -1)
+    open_rows = jnp.where((sub8 & 1) == 0, has_lower, has_upper) > 0
+    through = jnp.where(open_rows, through, -1)
+    direct = jnp.where(open_rows[0:2, :], direct, -1)
+    rows = [direct[0:1, :], direct[1:2, :]] + [through[i : i + 1, :] for i in range(2, 6)]
+    rows.append(jnp.where(lane_row < 64, t_row, -1))
+    for i, row in enumerate(rows):
+        at = slice(i * LANES, (i + 1) * LANES)
+        hot0[:, at] = jnp.where(column128 == rows_of(row, LANES), 1.0, 0.0).astype(BF16)
+        if i < 2:
+            hot1[:, at] = jnp.where(
+                column128 + LANES == rows_of(row, LANES), 1.0, 0.0
+            ).astype(BF16)
+    out_energy[:, 0:LANES] = energy[:, 0:LANES] * keep0
+    out_energy[:, LANES:] = energy[:, LANES:] * keep1
+    grad0 = first - own_sum[0]
+    grad1 = pltpu.roll(first, 4, 0) - own_sum[1]
+
+    for copy in backward:
         copy.wait_recv()
-
-    from_lower = jnp.where(s_me > 0, pltpu.roll(r_recv[0], 4, 0), 0.0)
-    from_upper = jnp.where(s_me < n_shock - 1, r_recv[1], 0.0)
-    back = jnp.concatenate([from_lower, from_upper], axis=1)
+    back = jnp.concatenate(
+        [
+            pltpu.roll(b_recv[slot(-1, 0)], 4, 0),
+            b_recv[slot(1, 0)],
+            pltpu.roll(b_recv[slot(-1, 1)], 4, 0),
+            b_recv[slot(1, 1)],
+            pltpu.roll(b_recv[slot(-1, -1)], 4, 0),
+            b_recv[slot(1, -1)],
+            between(b_recv[slot(0, 1)], b_recv[slot(0, -1)]),
+        ],
+        axis=1,
+    )
     back_hi = back.astype(BF16).astype(F32)
     back2 = jnp.concatenate([back_hi, back - back_hi], axis=0).astype(BF16)
-    added = mm_nt(back2, shock_hot[...])
-    added = added[0:8, :] + added[8:16, :]
-    u_send[...] = second + added[:, 2 * LANES : 3 * LANES]
-    for copy in u_copies:
-        copy.start()
-
-    first_swapped = pltpu.roll(first, 4, 0)
-    grad0 = first + added[:, 0:LANES] - own_sum[0]
-    grad1 = first_swapped + added[:, LANES : 2 * LANES] - own_sum[1]
-    force1 = -grad1[0:3, :]
-    half1 = half_velocity[:, LANES:]
-    out_disp[:, LANES:] = displaced[:, LANES:] * rows_of(keep1, 3)
-    out_vel[:, LANES:] = (half1 + kick_factor * force1) * rows_of(keep1, 3)
-    out_force[:, LANES:] = force1 * rows_of(keep1, 3)
-    out_energy[:, 0:LANES] = energy[:, 0:LANES] * keep0
-    out_energy[:, LANES:] = energy[:, LANES:] * keep1
-    out_disp[:, 0:LANES] = displaced[:, 0:LANES] * rows_of(keep0, 3)
-
-    for copy in u_copies:
-        copy.wait_recv()
-    merged = jnp.where(lane8 < 32, u_recv[1], jnp.where(lane8 < 64, u_recv[0], 0.0))
-    merged_hi = merged.astype(BF16).astype(F32)
-    merged2 = jnp.concatenate([merged_hi, merged - merged_hi], axis=0).astype(BF16)
-    added = mm_nt(merged2, trans_hot[...])
-    force0 = -(grad0 + added[0:8, :] + added[8:16, :])[0:3, :]
+    added0 = mm_nt(back2, hot0[...])
+    added1 = mm_nt(back2[:, 0 : 2 * LANES], hot1[...])
+    force0 = -(grad0 + added0[0:8, :] + added0[8:16, :])[0:3, :]
     velocity0 = half_velocity[:, 0:LANES] + kick_factor * force0
     ext[5, 0:3, :] = velocity0
     ext[6, 0:3, :] = force0
-    leave3 = rows_of(leave_row, 8)
+    leave8 = rows_of(leave_row, 8)
     for q, at in enumerate((0, 5, 6)):
-        v_send[q] = lane_gather(ext[at], leave3) * rows_of(sending, 8)
+        v_send[q] = lane_gather(ext[at], leave8) * rows_of(sending, 8)
     v_copy.start()
+    force1 = -(grad1 + added1[0:8, :] + added1[8:16, :])[0:3, :]
+    velocity1 = half_velocity[:, LANES:] + kick_factor * force1
     out_vel[:, 0:LANES] = velocity0 * rows_of(keep0, 3)
     out_force[:, 0:LANES] = force0 * rows_of(keep0, 3)
+    out_vel[:, LANES:] = velocity1 * rows_of(keep1, 3)
+    out_force[:, LANES:] = force1 * rows_of(keep1, 3)
+    for copy in (*forward, *backward):
+        copy.wait_send()
+    v_copy.wait_send()
     v_copy.wait_recv()
     for q in range(3):
         out_arr[q] = jnp.where(s_me < n_shock - 1, v_recv[q, 0:3, 0:16], 0.0)
-    for copy in (*t_copies, *s_copies, *r_copies, *u_copies, v_copy):
-        copy.wait_send()
+
+
+def kept(shape):
+    return pltpu.VMEM(shape, F32)
+
+
+def in_place(x):
+    return pltpu.with_memory_space_constraint(x, pltpu.VMEM)
+
+
+def finish(*refs):
+    for i in range(5):
+        refs[5 + i][...] = refs[i][...]
 
 
 def whole_step(n_shock, n_trans, *args):
     (disp, vel, force, beta, alpha, live, trans_idx, shock_idx, block, lane, leave, count) = args
     table = contraction_table()
-    vmem = pl.BlockSpec(memory_space=pltpu.VMEM)
-    smem = pl.BlockSpec(memory_space=pltpu.SMEM)
-    tile = (8, LANES)
-    outs = pl.pallas_call(
-        functools.partial(kernel, n_shock, n_trans),
-        out_shape=(
-            jax.ShapeDtypeStruct((3, 256), F32),
-            jax.ShapeDtypeStruct((3, 256), F32),
-            jax.ShapeDtypeStruct((3, 256), F32),
-            jax.ShapeDtypeStruct((1, 256), F32),
-            jax.ShapeDtypeStruct((3, 3, 16), F32),
-        ),
-        in_specs=[vmem] * 5 + [smem] + [vmem] * 5 + [smem] + [vmem] * 3,
-        out_specs=(vmem,) * 5,
-        scratch_shapes=[
-            pltpu.VMEM(tile, F32),
-            pltpu.VMEM((2, *tile), F32),
-            pltpu.VMEM(tile, F32),
-            pltpu.VMEM((2, *tile), F32),
-            pltpu.VMEM(tile, F32),
-            pltpu.VMEM((2, *tile), F32),
-            pltpu.VMEM(tile, F32),
-            pltpu.VMEM((2, *tile), F32),
-            pltpu.VMEM((3, *tile), F32),
-            pltpu.VMEM((3, *tile), F32),
-            pltpu.SemaphoreType.DMA((9,)),
-            pltpu.SemaphoreType.DMA((9,)),
-            pltpu.VMEM((7, *tile), F32),
-            pltpu.VMEM((ROWS, 256), jnp.int32),
-            pltpu.VMEM((ROWS, 256), jnp.int32),
-            pltpu.VMEM(tile, jnp.int32),
-            pltpu.VMEM((12, ROWS, 256), F32),
-            pltpu.VMEM((35, ROWS, 256), F32),
-            pltpu.VMEM((4 * MROWS, 256), F32),
-            pltpu.VMEM((4 * MROWS, 256), F32),
-            pltpu.VMEM((LANES, 26 * 256), BF16),
-            pltpu.VMEM((48, 26 * 256), BF16),
-            pltpu.VMEM((LANES, LANES), F32),
-            pltpu.VMEM((3 * LANES, 2 * LANES), BF16),
-            pltpu.VMEM((LANES, LANES), BF16),
-            pltpu.VMEM((3, ROWS, 256), F32),
-            pltpu.VMEM((2, *tile), F32),
-        ],
-        compiler_params=pltpu.CompilerParams(collective_id=0, has_side_effects=True),
-        name="whole_step",
-    )(
+    inputs = (
         disp,
         vel,
         force,
@@ -576,6 +609,60 @@
         jnp.asarray(table, BF16),
         jnp.asarray(table.T, BF16),
     )
+    vmem = pl.BlockSpec(memory_space=pltpu.VMEM)
+    tile = (8, LANES)
+    shapes = ((3, 256), (3, 256), (3, 256), (1, 256), (3, 3, 16))
+    outs = pl.pallas_call(
+        functools.partial(kernel, n_shock, n_trans),
+        out_shape=tuple(kept(shape) for shape in shapes),
+        in_specs=[pl.BlockSpec(memory_space=pltpu.HBM)] * N_IN,
+        out_specs=(vmem,) * 5,
+        scratch_shapes=[
+            (pltpu.SMEM if i in (5, 11) else pltpu.VMEM)(x.shape, x.dtype)
+            for i, x in enumerate(inputs)
+        ]
+        + [
+            pltpu.SemaphoreType.DMA((N_IN,)),
+            pltpu.VMEM(tile, F32),
+            pltpu.VMEM(tile, F32),
+            pltpu.VMEM((8, *tile), F32),
+            pltpu.VMEM(tile, F32),
+            pltpu.VMEM(tile, F32),
+            pltpu.VMEM((8, *tile), F32),
+            pltpu.VMEM((3, *tile), F32),
+            pltpu.VMEM((3, *tile), F32),
+            pltpu.SemaphoreType.DMA((8,)),
+            pltpu.SemaphoreType.DMA((8,)),
+            pltpu.SemaphoreType.DMA((8,)),
+            pltpu.SemaphoreType.DMA((8,)),
+            pltpu.SemaphoreType.DMA((2,)),
+            pltpu.VMEM((7, *tile), F32),
+            pltpu.VMEM((ROWS, 256), jnp.int32),
+            pltpu.VMEM((ROWS, 256), jnp.int32),
+            pltpu.VMEM(tile, jnp.int32),
+            pltpu.VMEM((3, ROWS, 256), F32),
+            pltpu.VMEM((12, ROWS, 256), F32),
+            pltpu.VMEM((35, ROWS, 256), F32),
+            pltpu.VMEM((4 * MROWS, 256), F32),
+            pltpu.VMEM((4 * MROWS, 256), F32),
+            pltpu.VMEM((LANES, 26 * 256), BF16),
+            pltpu.VMEM((LANES, LANES), F32),
+            pltpu.VMEM((LANES, 7 * LANES), BF16),
+            pltpu.VMEM((LANES, 2 * LANES), BF16),
+            pltpu.VMEM((3, ROWS, 256), F32),
+            pltpu.VMEM((2, *tile), F32),
+        ],
+        compiler_params=pltpu.CompilerParams(collective_id=0, has_side_effects=True),
+        name="whole_step",
+    )(*inputs)
+    outs = [in_place(x) for x in outs]
+    outs = pl.pallas_call(
+        finish,
+        out_shape=tuple(jax.ShapeDtypeStruct(shape, F32) for shape in shapes),
+        in_specs=[vmem] * 5,
+        out_specs=(vmem,) * 5,
+        name="finish",
+    )(*outs)
     return outs[0], outs[1], outs[2], outs[3].reshape(256), outs[4]
 
 

time: 37.7 us -> 27.4 us (0.73)
  the two profiles are of different devices: /device:TPU:99 before, /device:TPU:1 now
where the time goes in v2:
time: 27.4 us; the launch traced here: 27.3 us
  Pallas kernels  25.4 us (93%)
  between operations  1.94 us (7%)
    pallas_call x1, Pallas kernels, whole_step(): pl.pallas_call(functools.partial(kernel, n_shock, n_trans), out_shape=tup...  24.8 us
    pallas_call x1, Pallas kernels, whole_step(): pl.pallas_call(finish, out_shape=tuple((jax.ShapeDtypeStruct(shape, F32)...  0.61 us

profile of v2, /device:TPU:1, one launch (start us, length us, event | category | flops | bytes accessed | tf_op | source)
XLA Modules:
  0.0 27.3 jit_solution(1464336515138025055)
XLA Ops:
  1.9 24.8 %whole_step.1 = (f32[3,256]{1,0:T(4,128)S(1)}, f32[3,256]{1,0:T(4,128)S(1)}, f32[3,256]{1,0:T(4,128)S(1)}, f32[1,256]{1,0:T(1,128)S(1)}, f32[3,3,16]{2,1,0:T(4,128)S(1)}) custom-call(f32[3,256]{1,0:T(4,128)} %refs_0_.1, f32[3,256]{1,0:T(4,128)} %refs_1_.1, f32[3,256]{1,0:T(4,128)} %refs_2_.1, f32[1,50]{1,0:T(1,128)} %bitcast.3, f32[50,50]{1,0:T(8,128)} %refs_4_.1, ...), custom_call_target="tpu_custom_call" | custom-call | tf_op jit(solution)/shard_map/whole_step/pallas_call | solution.py:615
  26.7 0.6 %finish.1 = (f32[3,256]{1,0:T(4,128)}, f32[3,256]{1,0:T(4,128)}, f32[3,256]{1,0:T(4,128)}, f32[1,256]{1,0:T(1,128)}, f32[3,3,16]{2,1,0:T(4,128)}) custom-call(f32[3,256]{1,0:T(4,128)S(1)} %get-tuple-element.15.refs_0_, f32[3,256]{1,0:T(4,128)S(1)} %get-tuple-element.16.refs_1_, f32[3,256]{1,0:T(4,128)S(1)} %get-tuple-element.17.refs_2_, ...), custom_call_target="tpu_custom_call" | custom-call | tf_op jit(solution)/shard_map/finish/pallas_call | solution.py:659

commit v3 on v2

--- a/solution.py
+++ b/solution.py
@@ -126,7 +126,20 @@
     return r
 
 
-DIRS = ((0, 1), (0, -1), (1, 0), (-1, 0), (1, 1), (1, -1), (-1, 1), (-1, -1))
+DIRS = (
+    (1, 1),
+    (1, -1),
+    (-1, 1),
+    (-1, -1),
+    (0, 1),
+    (0, -1),
+    (1, 0),
+    (-1, 0),
+    (-2, 1),
+    (-2, -1),
+    (-2, 0),
+)
+NEAR = 8
 N_IN = 15
 
 
@@ -153,16 +166,20 @@
         t_send,
         s_send,
         f_recv,
-        u_send,
-        r_send,
+        m_send,
         b_recv,
-        v_send,
-        v_recv,
+        w_send,
+        w_recv,
+        c_send,
+        c_recv,
+        p_send,
+        p_recv,
         f_send_sems,
         f_recv_sems,
         b_send_sems,
         b_recv_sems,
-        v_sems,
+        x_send_sems,
+        x_recv_sems,
         ext,
         blk,
         lan,
@@ -176,6 +193,7 @@
         apad,
         hot0,
         hot1,
+        arr_hot,
         grads,
         own_sum,
     ) = refs[N_IN + 5 :]
@@ -212,9 +230,54 @@
             lax.rem(t_me + (dt + n_trans), n_trans),
         )
 
+    inside = {
+        -2: s_me > 1,
+        -1: s_me > 0,
+        0: None,
+        1: s_me < n_shock - 1,
+        2: s_me < n_shock - 2,
+    }
+
+    def where_inside(ds, action):
+        if inside[ds] is None:
+            action()
+        else:
+            pl.when(inside[ds])(action)
+
+    def clear(ds):
+        def action():
+            for dt in (-1, 0, 1):
+                k = DIRS.index((-ds, -dt))
+                b_recv[k] = jnp.zeros((2, 8, LANES), F32)
+                if k < NEAR:
+                    f_recv[k] = jnp.zeros((8, LANES), F32)
+            if ds == 1:
+                w_recv[...] = jnp.zeros((8, LANES), F32)
+                c_recv[...] = jnp.zeros((8, LANES), F32)
+                p_recv[...] = jnp.zeros((8, LANES), F32)
+
+        pl.when(jnp.logical_not(inside[ds]))(action)
+
+    for ds in (-1, 1, 2):
+        clear(ds)
+
     barrier = pltpu.get_barrier_semaphore()
-    for ds, dt in DIRS:
-        pl.semaphore_signal(barrier, inc=1, device_id=place(ds, dt), device_id_type=MESH)
+
+    def greet(ds):
+        def action():
+            for dt in (-1, 0, 1):
+                if (ds, dt) != (0, 0):
+                    pl.semaphore_signal(
+                        barrier, inc=1, device_id=place(ds, dt), device_id_type=MESH
+                    )
+
+        return action
+
+    for ds in (0, 1, -1, 2, -2):
+        where_inside(ds, greet(ds))
+    peers = 2
+    for ds in (1, -1, 2, -2):
+        peers = peers + jnp.where(inside[ds], 3, 0)
 
     def remote(src, dst, send_sem, recv_sem, where):
         return pltpu.make_async_remote_copy(
@@ -227,26 +290,69 @@
         )
 
     forward = [
-        remote(
-            s_send if dt == 0 else t_send,
-            f_recv.at[k],
-            f_send_sems.at[k],
-            f_recv_sems.at[k],
-            (ds, dt),
+        (
+            ds,
+            remote(
+                s_send if dt == 0 else t_send,
+                f_recv.at[k],
+                f_send_sems.at[k],
+                f_recv_sems.at[k],
+                (ds, dt),
+            ),
+        )
+        for k, (ds, dt) in enumerate(DIRS[:NEAR])
+    ]
+    backward = [
+        (
+            ds,
+            remote(
+                m_send if whole else m_send.at[0],
+                b_recv.at[k] if whole else b_recv.at[k, 0],
+                b_send_sems.at[k],
+                b_recv_sems.at[k],
+                (ds, dt),
+            ),
         )
         for k, (ds, dt) in enumerate(DIRS)
+        for whole in (dt != 0 and ds in (0, -1),)
     ]
-    backward = [
-        remote(
-            u_send if ds == 0 else r_send,
-            b_recv.at[k],
-            b_send_sems.at[k],
-            b_recv_sems.at[k],
-            (ds, dt),
-        )
-        for k, (ds, dt) in enumerate(DIRS)
+    extra = [
+        (-1, remote(src, dst, x_send_sems.at[i], x_recv_sems.at[i], (-1, 0)))
+        for i, (src, dst) in enumerate(((w_send, w_recv), (c_send, c_recv), (p_send, p_recv)))
     ]
-    v_copy = remote(v_send, v_recv, v_sems.at[0], v_sems.at[1], (-1, 0))
+
+    def start(copies):
+        for ds in (1, -1, 0, -2):
+            chosen = [copy for at, copy in copies if at == ds]
+
+            def action(chosen=chosen):
+                for copy in chosen:
+                    copy.start()
+
+            if chosen:
+                where_inside(ds, action)
+
+    def receive(copies):
+        for ds in (0, 1, -1, -2):
+            chosen = [copy for at, copy in copies if at == ds]
+
+            def action(chosen=chosen):
+                for copy in chosen:
+                    copy.wait_recv()
+
+            if chosen:
+                where_inside(-ds, action)
+
+    def drain(copies):
+        for ds in (0, 1, -1, -2):
+            chosen = [copy for at, copy in copies if at == ds]
+
+            def action(chosen=chosen):
+                for copy in chosen:
+                    copy.wait_send()
+
+            if chosen:
+                where_inside(ds, action)
 
     def slot(ds, dt):
         return DIRS.index((-ds, -dt))
@@ -254,12 +360,10 @@
     lane_row = lax.broadcasted_iota(jnp.int32, (1, LANES), 1)
     lane8 = lax.broadcasted_iota(jnp.int32, (8, LANES), 1)
     sub8 = lax.broadcasted_iota(jnp.int32, (8, LANES), 0)
-    has_lower = jnp.where(s_me > 0, 1, 0)
-    has_upper = jnp.where(s_me < n_shock - 1, 1, 0)
 
     idx_pad[...] = jnp.zeros_like(idx_pad)
     ext[...] = jnp.zeros_like(ext)
-    for i in (0, 1, 2, 6, 7):
+    for i in (0, 1, 2, 6, 7, 10, 11):
         loads[i].wait()
     half_velocity = vel[...] + kick_factor * force[...]
     displaced = disp[...] + drift_step * half_velocity
@@ -282,17 +386,24 @@
     )
     s_send[...] = jnp.where((sub8 & 3) == 3, shock8.astype(F32), s_own)
 
-    pl.semaphore_wait(barrier, len(DIRS))
-    for k in (4, 5, 6, 7, 0, 1, 2, 3):
-        forward[k].start()
-
-    for i in (8, 9, 10, 5, 11, 4, 3):
+    idx_pad[4:5, 0:16] = leave_idx[...]
+    leave_row = idx_pad[4:5, :]
+    sending = jnp.where(lane_row < leave_count[0], 1.0, 0.0)
+    for h in range(2):
+        ext[5 + h, 0:3, :] = half_velocity[:, h * LANES : (h + 1) * LANES]
+    leaving = jnp.where(sub8 < 4, ext[0], pltpu.roll(ext[5], 4, 0))
+    w_send[...] = lane_gather(leaving, rows_of(leave_row, 8)) * rows_of(sending, 8)
+
+    pl.semaphore_wait(barrier, peers)
+    start(forward)
+    start(extra[0:1])
+
+    for i in (8, 9, 5, 4, 3):
         loads[i].wait()
     blk[...] = jnp.full_like(blk, -1)
     lan[...] = jnp.zeros_like(lan)
     blk[0:26, :] = nb_block[...]
     lan[0:26, :] = nb_lane[...] & 127
-    idx_pad[4:5, 0:16] = leave_idx[...]
     column = lax.broadcasted_iota(jnp.int32, (LANES, 2 * LANES), 0)
 
     def fill_onehot(k, carry):
@@ -317,8 +428,6 @@
             )
 
     column128 = lax.broadcasted_iota(jnp.int32, (LANES, LANES), 0)
-    leave_row = idx_pad[4:5, :]
-    sending = jnp.where(lane_row < leave_count[0], 1.0, 0.0)
     leave_hot = jnp.where(column128 == rows_of(leave_row, LANES), 1.0, 0.0).astype(BF16)
     departed = mm_nt(rows_of(sending, 16).astype(BF16), leave_hot)[0:1, :]
     keep0 = jnp.where(lane_row < live[0], 1.0, 0.0) * (1.0 - departed)
@@ -337,8 +446,7 @@
     for n in range(4):
         mom[n * MROWS + 32 : (n + 1) * MROWS, :] = jnp.zeros((8, 2 * LANES), F32)
 
-    for copy in forward:
-        copy.wait_recv()
+    receive(forward)
 
     def between(lower, upper):
         return jnp.where(lane8 < 32, lower, jnp.where(lane8 < 64, upper, 0.0))
@@ -355,12 +463,23 @@
     )
     direct = jnp.where(sub8 < 4, pltpu.roll(from_low, 4, 0), pltpu.roll(from_up, 4, 0))
     both = jnp.where(lists >= 256, lane_gather(across, lists & 127), direct)
-    both = jnp.where(jnp.where(sub8 < 4, has_lower, has_upper) > 0, both, 0.0)
     turned = pltpu.roll(both, 64, 1)
     swapped = pltpu.roll(turned, 4, 0)
     ext[2] = jnp.where(lane8 < 64, t_ghost, turned)
     ext[3] = jnp.where(lane8 < 64, turned, swapped)
     ext[4] = swapped
+
+    table = jnp.where(
+        sub8 < 4, pltpu.roll(f_recv[slot(0, 1)], 6, 0), f_recv[slot(0, -1)]
+    ).astype(jnp.int32)
+    through = lane_gather(rows_of(t_row, 8), table & 127)
+    first_of = jnp.where(sub8 < 4, 256, 288)
+    through = jnp.where(table >= first_of, jnp.where(table < first_of + 32, through, -1), -1)
+    direct = idx_pad[2:4, :]
+    c_send[...] = through.astype(F32)
+    c_send[0:2, :] = jnp.where(direct < 256, direct, -1).astype(F32)
+    c_send[6:7, :] = jnp.where(lane_row < 64, t_row, -1).astype(F32)
+    c_send[7:8, :] = jnp.where(sending > 0.0, leave_row, -2).astype(F32)
 
     for h in range(2):
         hs = slice(h * LANES, (h + 1) * LANES)
@@ -500,30 +619,19 @@
     first = spread[0:8, :]
     second = spread[8:16, :]
     third = spread[16:24, :]
-    u_send[...] = second
     second_turned = pltpu.roll(second, 64, 1)
     third_turned = pltpu.roll(third, 64, 1)
     shifted = jnp.where(
         sub8 < 4, pltpu.roll(second_turned, 4, 0), pltpu.roll(third_turned, 4, 0)
     )
-    r_send[...] = jnp.where(lane8 < 64, second_turned, shifted)
-    for k in (4, 5, 6, 7, 0, 1, 2, 3):
-        backward[k].start()
-
-    t_row8 = rows_of(t_row, 8)
-    up_tile = f_recv[slot(0, 1)]
-    down_tile = f_recv[slot(0, -1)]
-    table = jnp.where(sub8 < 4, pltpu.roll(up_tile, 6, 0), down_tile).astype(jnp.int32)
-    through = lane_gather(t_row8, table & 127)
-    start = jnp.where(sub8 < 4, 256, 288)
-    through = jnp.where(table >= start, jnp.where(table < start + 32, through, -1), -1)
-    direct = idx_pad[2:4, :]
-    direct = jnp.where(direct < 256, direct, -1)
-    open_rows = jnp.where((sub8 & 1) == 0, has_lower, has_upper) > 0
-    through = jnp.where(open_rows, through, -1)
-    direct = jnp.where(open_rows[0:2, :], direct, -1)
-    rows = [direct[0:1, :], direct[1:2, :]] + [through[i : i + 1, :] for i in range(2, 6)]
-    rows.append(jnp.where(lane_row < 64, t_row, -1))
+    grad0 = first - own_sum[0]
+    m_send[1] = second
+    m_send[0] = jnp.where(lane8 < 64, second_turned, shifted)
+    p_send[...] = jnp.where(sub8 < 3, grad0, 0.0)
+    start(backward)
+    start(extra[1:3])
+
+    rows = [c_send[i : i + 1, :].astype(jnp.int32) for i in range(7)]
     for i, row in enumerate(rows):
         at = slice(i * LANES, (i + 1) * LANES)
         hot0[:, at] = jnp.where(column128 == rows_of(row, LANES), 1.0, 0.0).astype(BF16)
@@ -533,47 +641,73 @@
             ).astype(BF16)
     out_energy[:, 0:LANES] = energy[:, 0:LANES] * keep0
     out_energy[:, LANES:] = energy[:, LANES:] * keep1
-    grad0 = first - own_sum[0]
     grad1 = pltpu.roll(first, 4, 0) - own_sum[1]
 
-    for copy in backward:
-        copy.wait_recv()
-    back = jnp.concatenate(
-        [
-            pltpu.roll(b_recv[slot(-1, 0)], 4, 0),
-            b_recv[slot(1, 0)],
-            pltpu.roll(b_recv[slot(-1, 1)], 4, 0),
-            b_recv[slot(1, 1)],
-            pltpu.roll(b_recv[slot(-1, -1)], 4, 0),
-            b_recv[slot(1, -1)],
-            between(b_recv[slot(0, 1)], b_recv[slot(0, -1)]),
-        ],
-        axis=1,
-    )
-    back_hi = back.astype(BF16).astype(F32)
-    back2 = jnp.concatenate([back_hi, back - back_hi], axis=0).astype(BF16)
-    added0 = mm_nt(back2, hot0[...])
-    added1 = mm_nt(back2[:, 0 : 2 * LANES], hot1[...])
+    receive(extra[0:2])
+    slots = rows_of(c_recv[7:8, :], LANES).T[0:16, :]
+    for i in range(8):
+        row = lane_row.astype(F32) if i == 7 else c_recv[i : i + 1, :]
+        arr_hot[:, i * LANES : (i + 1) * LANES] = jnp.where(
+            rows_of(row, 16) == slots, 1.0, 0.0
+        ).astype(BF16)
+
+    receive(backward)
+    receive(extra[2:3])
+
+    def lower_of(ds, dt):
+        return b_recv[slot(ds, dt), 0]
+
+    def upper_of(ds, dt):
+        return pltpu.roll(b_recv[slot(ds, dt), 0], 4, 0)
+
+    def pieces_of(tiles):
+        back = jnp.concatenate([jnp.where(sub8 < 3, tile, 0.0) for tile in tiles], axis=1)
+        hi = back.astype(BF16).astype(F32)
+        return jnp.concatenate([hi, back - hi], axis=0).astype(BF16)
+
+    back = pieces_of(
+        (
+            upper_of(-1, 0),
+            lower_of(1, 0),
+            upper_of(-1, 1),
+            lower_of(1, 1),
+            upper_of(-1, -1),
+            lower_of(1, -1),
+            between(b_recv[slot(0, 1), 1], b_recv[slot(0, -1), 1]),
+        )
+    )
+    added0 = mm_nt(back, hot0[...])
+    added1 = mm_nt(back[:, 0 : 2 * LANES], hot1[...])
+    arriving = pieces_of(
+        (
+            pltpu.roll(m_send[0], 4, 0),
+            lower_of(2, 0),
+            upper_of(0, 1),
+            lower_of(2, 1),
+            upper_of(0, -1),
+            lower_of(2, -1),
+            between(b_recv[slot(1, 1), 1], b_recv[slot(1, -1), 1]),
+            p_recv[...],
+        )
+    )
+    added2 = mm_nt(arriving, arr_hot[...])
     force0 = -(grad0 + added0[0:8, :] + added0[8:16, :])[0:3, :]
     velocity0 = half_velocity[:, 0:LANES] + kick_factor * force0
-    ext[5, 0:3, :] = velocity0
-    ext[6, 0:3, :] = force0
-    leave8 = rows_of(leave_row, 8)
-    for q, at in enumerate((0, 5, 6)):
-        v_send[q] = lane_gather(ext[at], leave8) * rows_of(sending, 8)
-    v_copy.start()
     force1 = -(grad1 + added1[0:8, :] + added1[8:16, :])[0:3, :]
     velocity1 = half_velocity[:, LANES:] + kick_factor * force1
+    force2 = -(added2[0:8, :] + added2[8:16, :])[0:3, :]
+    state = w_recv[...]
     out_vel[:, 0:LANES] = velocity0 * rows_of(keep0, 3)
     out_force[:, 0:LANES] = force0 * rows_of(keep0, 3)
     out_vel[:, LANES:] = velocity1 * rows_of(keep1, 3)
     out_force[:, LANES:] = force1 * rows_of(keep1, 3)
-    for copy in (*forward, *backward):
-        copy.wait_send()
-    v_copy.wait_send()
-    v_copy.wait_recv()
-    for q in range(3):
-        out_arr[q] = jnp.where(s_me < n_shock - 1, v_recv[q, 0:3, 0:16], 0.0)
+    for q, value in enumerate(
+        (state[0:3, 0:16], state[4:7, 0:16] + kick_factor * force2, force2)
+    ):
+        out_arr[q] = jnp.where(s_me < n_shock - 1, value, 0.0)
+    drain(forward)
+    drain(backward)
+    drain(extra)
 
 
 def kept(shape):
@@ -625,17 +759,21 @@
             pltpu.SemaphoreType.DMA((N_IN,)),
             pltpu.VMEM(tile, F32),
             pltpu.VMEM(tile, F32),
-            pltpu.VMEM((8, *tile), F32),
+            pltpu.VMEM((NEAR, *tile), F32),
+            pltpu.VMEM((2, *tile), F32),
+            pltpu.VMEM((len(DIRS), 2, *tile), F32),
             pltpu.VMEM(tile, F32),
             pltpu.VMEM(tile, F32),
-            pltpu.VMEM((8, *tile), F32),
-            pltpu.VMEM((3, *tile), F32),
-            pltpu.VMEM((3, *tile), F32),
-            pltpu.SemaphoreType.DMA((8,)),
-            pltpu.SemaphoreType.DMA((8,)),
-            pltpu.SemaphoreType.DMA((8,)),
-            pltpu.SemaphoreType.DMA((8,)),
-            pltpu.SemaphoreType.DMA((2,)),
+            pltpu.VMEM(tile, F32),
+            pltpu.VMEM(tile, F32),
+            pltpu.VMEM(tile, F32),
+            pltpu.VMEM(tile, F32),
+            pltpu.SemaphoreType.DMA((NEAR,)),
+            pltpu.SemaphoreType.DMA((NEAR,)),
+            pltpu.SemaphoreType.DMA((len(DIRS),)),
+            pltpu.SemaphoreType.DMA((len(DIRS),)),
+            pltpu.SemaphoreType.DMA((3,)),
+            pltpu.SemaphoreType.DMA((3,)),
             pltpu.VMEM((7, *tile), F32),
             pltpu.VMEM((ROWS, 256), jnp.int32),
             pltpu.VMEM((ROWS, 256), jnp.int32),
@@ -649,6 +787,7 @@
             pltpu.VMEM((LANES, LANES), F32),
             pltpu.VMEM((LANES, 7 * LANES), BF16),
             pltpu.VMEM((LANES, 2 * LANES), BF16),
+            pltpu.VMEM((16, 8 * LANES), BF16),
             pltpu.VMEM((3, ROWS, 256), F32),
             pltpu.VMEM((2, *tile), F32),
         ],

time: 27.4 us -> 23.3 us (0.85)
  the two profiles are of different devices: /device:TPU:1 before, /device:TPU:96 now
where the time goes in v3:
time: 23.3 us; the launch traced here: 23.2 us
  Pallas kernels  21.2 us (91%)
  between operations  1.94 us (8%)
    pallas_call x1, Pallas kernels, whole_step(): pl.pallas_call(functools.partial(kernel, n_shock, n_trans), out_shape=tup...  20.6 us
    pallas_call x1, Pallas kernels, whole_step(): pl.pallas_call(finish, out_shape=tuple((jax.ShapeDtypeStruct(shape, F32)...  0.61 us

profile of v3, /device:TPU:96, one launch (start us, length us, event | category | flops | bytes accessed | tf_op | source)
XLA Modules:
  0.0 23.2 jit_solution(5001385434451446718)
XLA Ops:
  1.9 20.6 %whole_step.1 = (f32[3,256]{1,0:T(4,128)S(1)}, f32[3,256]{1,0:T(4,128)S(1)}, f32[3,256]{1,0:T(4,128)S(1)}, f32[1,256]{1,0:T(1,128)S(1)}, f32[3,3,16]{2,1,0:T(4,128)S(1)}) custom-call(f32[3,256]{1,0:T(4,128)} %refs_0_.1, f32[3,256]{1,0:T(4,128)} %refs_1_.1, f32[3,256]{1,0:T(4,128)} %refs_2_.1, f32[1,50]{1,0:T(1,128)} %bitcast.3, f32[50,50]{1,0:T(8,128)} %refs_4_.1, ...), custom_call_target="tpu_custom_call" | custom-call | tf_op jit(solution)/shard_map/whole_step/pallas_call | solution.py:749
  22.6 0.6 %finish.1 = (f32[3,256]{1,0:T(4,128)}, f32[3,256]{1,0:T(4,128)}, f32[3,256]{1,0:T(4,128)}, f32[1,256]{1,0:T(1,128)}, f32[3,3,16]{2,1,0:T(4,128)}) custom-call(f32[3,256]{1,0:T(4,128)S(1)} %get-tuple-element.15.refs_0_, f32[3,256]{1,0:T(4,128)S(1)} %get-tuple-element.16.refs_1_, f32[3,256]{1,0:T(4,128)S(1)} %get-tuple-element.17.refs_2_, ...), custom_call_target="tpu_custom_call" | custom-call | tf_op jit(solution)/shard_map/finish/pallas_call | solution.py:798

commit v4 on v3

--- a/solution.py
+++ b/solution.py
@@ -21,7 +21,8 @@
 moment_scale = 0.25
 pair_list = ((0, 0), (0, 1), (0, 2), (0, 3), (1, 1), (1, 2), (1, 3), (2, 2), (2, 3), (3, 3))
 LANES = 128
-ROWS = 32
+ROWS = 56
+CHUNKS = ((0, 16), (16, 32), (32, 48), (48, 56))
 MROWS = 40
 DROWS = 64
 
@@ -37,6 +38,13 @@
 
 TRIPLES = exponents()
 INDEX = {t: i for i, t in enumerate(TRIPLES)}
+BASIS = [t for t in TRIPLES if t[2] < 2]
+PLACE = {t: i for i, t in enumerate(BASIS)}
+
+
+def reduced(t):
+    p, q, w = t
+    return (p, q, w - 2), (p + 2, q, w - 2), (p, q + 2, w - 2)
 
 
 def lattice_rows():
@@ -58,9 +66,9 @@
                 vector[others[0]] = leading
                 vector[others[1]] = trailing
                 entries.append(vector)
-    while len(entries) < ROWS:
+    while len(entries) < ROWS // 2:
         entries.append([1.0, 1.0, 1.0])
-    table = np.array(entries, dtype=np.float32).T
+    table = np.repeat(np.array(entries, dtype=np.float32), 2, axis=0).T
     return np.broadcast_to(table[:, :, None], (3, ROWS, LANES)).copy()
 
 
@@ -108,6 +116,25 @@
 
 def rows_of(row, count):
     return jnp.broadcast_to(row, (count, row.shape[1]))
+
+
+def over(tile, count):
+    return jnp.concatenate([tile] * count, axis=0) if count > 1 else tile
+
+
+def row_sums(x):
+    total = x[0:8, :]
+    for i in range(8, x.shape[0], 8):
+        total = total + x[i : i + 8, :]
+    total = total + pltpu.roll(total, 4, 0)
+    return total + pltpu.roll(total, 2, 0)
+
+
+def horner(x, value, slope, term):
+    if value is None:
+        return term, None
+    slope = value if slope is None else slope * x + value
+    return value * x + term, slope
 
 
 def sin_of(u):
@@ -140,25 +167,24 @@
     (-2, 0),
 )
 NEAR = 8
-N_IN = 15
+N_IN = 13
 
 
 def kernel(n_shock, n_trans, *refs):
     hbm = refs[:N_IN]
-    out_disp, out_vel, out_force, out_energy, out_arr = refs[N_IN : N_IN + 5]
+    live, leave_count = refs[N_IN : N_IN + 2]
+    out_disp, out_vel, out_force, out_energy, out_arr = refs[N_IN + 2 : N_IN + 7]
     (
         disp,
         vel,
         force,
         beta,
         alpha,
-        live,
         trans_idx,
         shock_idx,
         nb_block,
         nb_lane,
         leave_idx,
-        leave_count,
         offs,
         wmat,
         wmat_t,
@@ -186,7 +212,7 @@
         idx_pad,
         near_own,
         geom,
-        monos,
+        tiles,
         mom,
         dmom,
         onehot,
@@ -196,20 +222,18 @@
         arr_hot,
         grads,
         own_sum,
-    ) = refs[N_IN + 5 :]
+    ) = refs[N_IN + 7 :]
     local = (
         disp,
         vel,
         force,
         beta,
         alpha,
-        live,
         trans_idx,
         shock_idx,
         nb_block,
         nb_lane,
         leave_idx,
-        leave_count,
         offs,
         wmat,
         wmat_t,
@@ -218,17 +242,17 @@
         pltpu.make_async_copy(src, dst, in_sems.at[i])
         for i, (src, dst) in enumerate(zip(hbm, local, strict=True))
     ]
-    for i in (0, 1, 2, 6, 7, 8, 9, 10, 5, 11, 4, 3, 12, 13, 14):
-        loads[i].start()
-
     s_me = lax.axis_index("shock")
     t_me = lax.axis_index("trans")
 
+    t_near = {
+        -1: jnp.where(t_me > 0, t_me - 1, n_trans - 1),
+        0: t_me,
+        1: jnp.where(t_me < n_trans - 1, t_me + 1, 0),
+    }
+
     def place(ds, dt):
-        return (
-            lax.rem(s_me + (ds + n_shock), n_shock),
-            lax.rem(t_me + (dt + n_trans), n_trans),
-        )
+        return s_me + ds, t_near[dt]
 
     inside = {
         -2: s_me > 1,
@@ -258,9 +282,6 @@
 
         pl.when(jnp.logical_not(inside[ds]))(action)
 
-    for ds in (-1, 1, 2):
-        clear(ds)
-
     barrier = pltpu.get_barrier_semaphore()
 
     def greet(ds):
@@ -275,6 +296,8 @@
 
     for ds in (0, 1, -1, 2, -2):
         where_inside(ds, greet(ds))
+    for i in (0, 1, 2, 5, 6, 7, 8, 9, 4, 3, 10, 11, 12):
+        loads[i].start()
     peers = 2
     for ds in (1, -1, 2, -2):
         peers = peers + jnp.where(inside[ds], 3, 0)
@@ -363,7 +386,7 @@
 
     idx_pad[...] = jnp.zeros_like(idx_pad)
     ext[...] = jnp.zeros_like(ext)
-    for i in (0, 1, 2, 6, 7, 10, 11):
+    for i in (0, 1, 2, 5, 6):
         loads[i].wait()
     half_velocity = vel[...] + kick_factor * force[...]
     displaced = disp[...] + drift_step * half_velocity
@@ -386,6 +409,12 @@
     )
     s_send[...] = jnp.where((sub8 & 3) == 3, shock8.astype(F32), s_own)
 
+    pl.semaphore_wait(barrier, peers)
+    start(forward)
+    for ds in (-1, 1, 2):
+        clear(ds)
+
+    loads[9].wait()
     idx_pad[4:5, 0:16] = leave_idx[...]
     leave_row = idx_pad[4:5, :]
     sending = jnp.where(lane_row < leave_count[0], 1.0, 0.0)
@@ -393,41 +422,42 @@
         ext[5 + h, 0:3, :] = half_velocity[:, h * LANES : (h + 1) * LANES]
     leaving = jnp.where(sub8 < 4, ext[0], pltpu.roll(ext[5], 4, 0))
     w_send[...] = lane_gather(leaving, rows_of(leave_row, 8)) * rows_of(sending, 8)
-
-    pl.semaphore_wait(barrier, peers)
-    start(forward)
     start(extra[0:1])
 
-    for i in (8, 9, 5, 4, 3):
+    for i in (7, 8, 4, 3):
         loads[i].wait()
     blk[...] = jnp.full_like(blk, -1)
     lan[...] = jnp.zeros_like(lan)
-    blk[0:26, :] = nb_block[...]
-    lan[0:26, :] = nb_lane[...] & 127
-    column = lax.broadcasted_iota(jnp.int32, (LANES, 2 * LANES), 0)
-
-    def fill_onehot(k, carry):
-        row = lan[pl.ds(k, 1), :]
-        hot = jnp.where(column == rows_of(row, LANES), 1.0, 0.0).astype(BF16)
-        onehot[:, pl.ds(pl.multiple_of(k * 2 * LANES, 2 * LANES), 2 * LANES)] = hot
-        return carry
-
-    lax.fori_loop(0, 26, fill_onehot, 0)
-    for i in (12, 13, 14):
-        loads[i].wait()
     for h in range(2):
         hs = slice(h * LANES, (h + 1) * LANES)
-        for c in range(3):
-            found = offs[c] - rows_of(ext[h, c : c + 1, :], ROWS)
-            parts = [
-                lane_gather(rows_of(ext[b, c : c + 1, :], ROWS), lan[:, hs]) for b in range(2)
-            ]
-            block = blk[:, hs]
-            near_own[c, :, hs] = found + jnp.where(
-                block == 0, parts[0], jnp.where(block == 1, parts[1], 0.0)
-            )
+        blk[pl.ds(h, 26, stride=2), :] = nb_block[:, hs]
+        lan[pl.ds(h, 26, stride=2), :] = nb_lane[:, hs] & 127
 
     column128 = lax.broadcasted_iota(jnp.int32, (LANES, LANES), 0)
+
+    def fill_onehot(k, carry):
+        for h in range(2):
+            row = lan[pl.ds(2 * k + h, 1), :]
+            hot = jnp.where(column128 == rows_of(row, LANES), 1.0, 0.0).astype(BF16)
+            at = pl.multiple_of((2 * k + h) * LANES, LANES)
+            onehot[:, pl.ds(at, LANES)] = hot
+        return carry
+
+    lax.fori_loop(0, 26, fill_onehot, 0)
+    for i in (10, 11, 12):
+        loads[i].wait()
+    even = (sub8 & 1) == 0
+    block = blk[...]
+    lane = lan[...]
+    for c in range(3):
+        own = jnp.where(even, rows_of(ext[0, c : c + 1, :], 8), rows_of(ext[1, c : c + 1, :], 8))
+        parts = [lane_gather(rows_of(ext[b, c : c + 1, :], ROWS), lane) for b in range(2)]
+        near_own[c] = (
+            offs[c]
+            - over(own, ROWS // 8)
+            + jnp.where(block == 0, parts[0], jnp.where(block == 1, parts[1], 0.0))
+        )
+
     leave_hot = jnp.where(column128 == rows_of(leave_row, LANES), 1.0, 0.0).astype(BF16)
     departed = mm_nt(rows_of(sending, 16).astype(BF16), leave_hot)[0:1, :]
     keep0 = jnp.where(lane_row < live[0], 1.0, 0.0) * (1.0 - departed)
@@ -481,58 +511,63 @@
     c_send[6:7, :] = jnp.where(lane_row < 64, t_row, -1).astype(F32)
     c_send[7:8, :] = jnp.where(sending > 0.0, leave_row, -2).astype(F32)
 
-    for h in range(2):
-        hs = slice(h * LANES, (h + 1) * LANES)
-        block = blk[:, hs]
-        lane = lan[:, hs]
-        parts = []
-        for c in range(3):
-            found = jnp.zeros((ROWS, LANES), F32)
-            for b in range(2, 5):
-                value = lane_gather(rows_of(ext[b, c : c + 1, :], ROWS), lane)
-                found = jnp.where(block == b, value, found)
-            parts.append(near_own[c, :, hs] + found)
-        px, py, pz = parts
-        square = px * px + py * py + pz * pz
-        inverse = lax.rsqrt(square)
-        distance = square * inverse
-        ux, uy, uz = px * inverse, py * inverse, pz * inverse
-        angle = (0.5 * math.pi) - (0.5 * math.pi / cutoff_radius) * distance
-        sine, cosine = sin_of(angle), cos_of(angle)
-        scale = jnp.where(block >= 0, moment_scale, 0.0)
-        smooth = scale * sine * sine
-        slope = scale * (-math.pi / cutoff_radius) * sine * cosine
-        radial = []
-        for n, center in enumerate(radial_centers):
-            z = (distance - center) * (1.0 / radial_width)
-            e = jnp.exp(-(z * z))
-            r = smooth * e
-            radial.append(r)
-            geom[n, :, hs] = r
-            geom[4 + n, :, hs] = slope * e - (2.0 / radial_width) * z * r
-        geom[8, :, hs] = ux
-        geom[9, :, hs] = uy
-        geom[10, :, hs] = uz
-        geom[11, :, hs] = inverse
-        values = {}
-        for m, (p, q, w) in enumerate(TRIPLES):
-            if m == 0:
-                value = None
-            elif p > 0:
-                prior = values[(p - 1, q, w)]
-                value = ux if prior is None else prior * ux
+    block = blk[...]
+    lane = lan[...]
+    parts = []
+    for c in range(3):
+        found = jnp.zeros((ROWS, LANES), F32)
+        for b in range(2, 5):
+            value = lane_gather(rows_of(ext[b, c : c + 1, :], ROWS), lane)
+            found = jnp.where(block == b, value, found)
+        parts.append(near_own[c] + found)
+    px, py, pz = parts
+    square = px * px + py * py + pz * pz
+    inverse = lax.rsqrt(square)
+    distance = square * inverse
+    ux, uy, uz = px * inverse, py * inverse, pz * inverse
+    angle = (0.5 * math.pi) - (0.5 * math.pi / cutoff_radius) * distance
+    sine, cosine = sin_of(angle), cos_of(angle)
+    scale = jnp.where(block >= 0, moment_scale, 0.0)
+    smooth = scale * sine * sine
+    slope = scale * (-math.pi / cutoff_radius) * sine * cosine
+    radial = []
+    for n, center in enumerate(radial_centers):
+        z = (distance - center) * (1.0 / radial_width)
+        e = jnp.exp(-(z * z))
+        r = smooth * e
+        radial.append(r)
+        geom[n] = r
+        geom[4 + n] = slope * e - (2.0 / radial_width) * z * r
+    geom[8] = ux
+    geom[9] = uy
+    geom[10] = uz
+    geom[11] = inverse
+    values = {}
+    sums = {}
+    for t in TRIPLES:
+        p, q, w = t
+        m = INDEX[t]
+        if w > 1:
+            low, left, right = reduced(t)
+            for n in range(4):
+                sums[(n, t)] = sums[(n, low)] - sums[(n, left)] - sums[(n, right)]
+        else:
+            if p > 0:
+                prior, factor = values[(p - 1, q, w)], ux
             elif q > 0:
-                prior = values[(p, q - 1, w)]
-                value = uy if prior is None else prior * uy
+                prior, factor = values[(p, q - 1, w)], uy
+            elif w > 0:
+                prior, factor = values[(p, q, w - 1)], uz
             else:
-                prior = values[(p, q, w - 1)]
-                value = uz if prior is None else prior * uz
-            values[(p, q, w)] = value
-            if value is not None:
-                monos[m, :, hs] = value
+                prior, factor = None, None
+            value = factor if prior is None else prior * factor
+            values[t] = value
             for n in range(4):
-                term = radial[n] if value is None else radial[n] * value
-                mom[n * MROWS + m : n * MROWS + m + 1, hs] = jnp.sum(term, axis=0, keepdims=True)
+                sums[(n, t)] = row_sums(radial[n] if value is None else radial[n] * value)
+        for n in range(4):
+            at = n * MROWS + m
+            mom[at : at + 1, 0:LANES] = sums[(n, t)][0:1, :]
+            mom[at : at + 1, LANES:] = sums[(n, t)][1:2, :]
 
     moments = [mom[n * MROWS : (n + 1) * MROWS, :] for n in range(4)]
     products = jnp.concatenate([moments[n] * moments[o] for n, o in pair_list], axis=0)
@@ -558,63 +593,95 @@
             total = part if total is None else total + part
         dmom[n * MROWS : (n + 1) * MROWS, :] = total
 
-    for h in range(2):
-        hs = slice(h * LANES, (h + 1) * LANES)
-        radial = [geom[n, :, hs] for n in range(4)]
-        dradial = [None] * 4
-        sums = {}
-        for m, (p, q, w) in enumerate(TRIPLES):
-            coefficient = None
-            for n in range(4):
-                row = rows_of(dmom[n * MROWS + m : n * MROWS + m + 1, hs], ROWS)
-                term = row if m == 0 else row * monos[m, :, hs]
-                dradial[n] = term if dradial[n] is None else dradial[n] + term
-                if m > 0:
-                    term = row * radial[n]
-                    coefficient = term if coefficient is None else coefficient + term
-            if m == 0:
-                continue
-            for c, (power, prior) in enumerate(
-                ((p, (p - 1, q, w)), (q, (p, q - 1, w)), (w, (p, q, w - 1)))
-            ):
-                if power == 0:
-                    continue
-                at = INDEX[prior]
-                term = coefficient if at == 0 else coefficient * monos[at, :, hs]
-                key = (c, power)
-                sums[key] = term if key not in sums else sums[key] + term
-        unit = [geom[8 + c, :, hs] for c in range(3)]
-        inverse = geom[11, :, hs]
+    for n in range(4):
+        slopes = {}
+        for t in TRIPLES:
+            at = n * MROWS + INDEX[t]
+            slopes[t] = jnp.where(
+                even,
+                rows_of(dmom[at : at + 1, 0:LANES], 8),
+                rows_of(dmom[at : at + 1, LANES:], 8),
+            )
+        for t in sorted(TRIPLES, key=lambda t: -t[2]):
+            if t[2] > 1:
+                low, left, right = reduced(t)
+                slopes[low] = slopes[low] + slopes[t]
+                slopes[left] = slopes[left] - slopes[t]
+                slopes[right] = slopes[right] - slopes[t]
+        for t in BASIS:
+            tiles[n * len(BASIS) + PLACE[t]] = slopes[t]
+
+    part8 = sub8 & 3
+    half_block = sub8 >> 2
+    spread = jnp.zeros((48, LANES), F32)
+    own_total = [None] * 3
+    for begin, end in CHUNKS:
+        count = (end - begin) // 8
+        at = slice(begin, end)
+        radial = [geom[n, at, :] for n in range(4)]
+        unit = [geom[8 + c, at, :] for c in range(3)]
+        ux, uy, uz = unit
+        found = []
+        for w in range(2):
+            size = 4 - w
+            value_x = slope_x = slope_y = None
+            heights = [None] * 4
+            for p in range(size, -1, -1):
+                value = slope = None
+                rows = [None] * 4
+                for q in range(size - p, -1, -1):
+                    coefficient = None
+                    for n in range(4):
+                        b = over(tiles[n * len(BASIS) + PLACE[(p, q, w)]], count)
+                        rows[n] = b if rows[n] is None else rows[n] * uy + b
+                        term = b * radial[n]
+                        coefficient = term if coefficient is None else coefficient + term
+                    value, slope = horner(uy, value, slope, coefficient)
+                for n in range(4):
+                    heights[n] = rows[n] if heights[n] is None else heights[n] * ux + rows[n]
+                value_x, slope_x = horner(ux, value_x, slope_x, value)
+                if slope is not None:
+                    slope_y = slope if slope_y is None else slope_y * ux + slope
+            found.append((value_x, slope_x, slope_y, heights))
+        inverse = geom[11, at, :]
+        tangent = [
+            (found[0][1] + uz * found[1][1]) * inverse,
+            (found[0][2] + uz * found[1][2]) * inverse,
+            found[1][0] * inverse,
+        ]
         along = None
         for n in range(4):
-            term = geom[4 + n, :, hs] * dradial[n]
+            term = geom[4 + n, at, :] * (found[0][3][n] + uz * found[1][3][n])
             along = term if along is None else along + term
-        tangent = []
-        for c in range(3):
-            total = sums[(c, 1)]
-            for power in (2, 3, 4):
-                total = total + float(power) * sums[(c, power)]
-            tangent.append(total * inverse)
-        inner = unit[0] * tangent[0] + unit[1] * tangent[1] + unit[2] * tangent[2]
-        along = along - inner
+        along = along - (ux * tangent[0] + uy * tangent[1] + uz * tangent[2])
         for c in range(3):
             g = tangent[c] + unit[c] * along
-            grads[c, :, hs] = g
-            own_sum[h, c : c + 1, :] = jnp.sum(g, axis=0, keepdims=True)
-
-    sub24 = lax.broadcasted_iota(jnp.int32, (24, 2 * LANES), 0)
-    row_block = sub24 >> 2
-    row_part = sub24 & 3
-    spread = jnp.zeros((48, LANES), F32)
-    for k in range(26):
-        gx = rows_of(grads[0, k : k + 1, :], 24)
-        gy = rows_of(grads[1, k : k + 1, :], 24)
-        gz = rows_of(grads[2, k : k + 1, :], 24)
-        value = jnp.where(row_part == 0, gx, jnp.where(row_part == 1, gy, gz))
-        value = jnp.where(row_block == rows_of(blk[k : k + 1, :], 24), value, 0.0)
-        hi = value.astype(BF16).astype(F32)
-        pieces = jnp.concatenate([hi, value - hi], axis=0).astype(BF16)
-        spread = spread + mm_nt(pieces, onehot[:, k * 2 * LANES : (k + 1) * 2 * LANES])
+            grads[c, at, :] = g
+            for i in range(count):
+                row = g[8 * i : 8 * i + 8, :]
+                own_total[c] = row if own_total[c] is None else own_total[c] + row
+        columns = []
+        for r in range(begin, min(end, 52)):
+            gx, gy, gz = (rows_of(grads[c, r : r + 1, :], 8) for c in range(3))
+            value = jnp.where(part8 == 0, gx, jnp.where(part8 == 1, gy, gz))
+            hi = value.astype(BF16).astype(F32)
+            lo = value - hi
+            place_of = rows_of(blk[r : r + 1, :], 8) - half_block
+            masks = [place_of == 2 * i for i in range(3)]
+            columns.append(
+                jnp.concatenate(
+                    [jnp.where(mask, x, 0.0) for x in (hi, lo) for mask in masks], axis=0
+                ).astype(BF16)
+            )
+        last = min(end, 52)
+        spread = spread + mm_nt(
+            jnp.concatenate(columns, axis=1), onehot[:, begin * LANES : last * LANES]
+        )
+    for c in range(3):
+        total = own_total[c] + pltpu.roll(own_total[c], 4, 0)
+        total = total + pltpu.roll(total, 2, 0)
+        for h in range(2):
+            own_sum[h, c : c + 1, :] = total[h : h + 1, :]
     spread = spread[0:24, :] + spread[24:48, :]
     first = spread[0:8, :]
     second = spread[8:16, :]
@@ -732,13 +799,11 @@
         force,
         beta.reshape(1, 50),
         alpha,
-        live,
         trans_idx,
         shock_idx,
         block,
         lane,
         leave.reshape(1, 16),
-        count,
         jnp.asarray(lattice_rows()),
         jnp.asarray(table, BF16),
         jnp.asarray(table.T, BF16),
@@ -749,11 +814,11 @@
     outs = pl.pallas_call(
         functools.partial(kernel, n_shock, n_trans),
         out_shape=tuple(kept(shape) for shape in shapes),
-        in_specs=[pl.BlockSpec(memory_space=pltpu.HBM)] * N_IN,
+        in_specs=[pl.BlockSpec(memory_space=pltpu.HBM)] * N_IN
+        + [pl.BlockSpec(memory_space=pltpu.SMEM)] * 2,
         out_specs=(vmem,) * 5,
         scratch_shapes=[
-            (pltpu.SMEM if i in (5, 11) else pltpu.VMEM)(x.shape, x.dtype)
-            for i, x in enumerate(inputs)
+            pltpu.VMEM(x.shape, x.dtype) for x in inputs
         ]
         + [
             pltpu.SemaphoreType.DMA((N_IN,)),
@@ -775,12 +840,12 @@
             pltpu.SemaphoreType.DMA((3,)),
             pltpu.SemaphoreType.DMA((3,)),
             pltpu.VMEM((7, *tile), F32),
-            pltpu.VMEM((ROWS, 256), jnp.int32),
-            pltpu.VMEM((ROWS, 256), jnp.int32),
+            pltpu.VMEM((ROWS, LANES), jnp.int32),
+            pltpu.VMEM((ROWS, LANES), jnp.int32),
             pltpu.VMEM(tile, jnp.int32),
-            pltpu.VMEM((3, ROWS, 256), F32),
-            pltpu.VMEM((12, ROWS, 256), F32),
-            pltpu.VMEM((35, ROWS, 256), F32),
+            pltpu.VMEM((3, ROWS, LANES), F32),
+            pltpu.VMEM((12, ROWS, LANES), F32),
+            pltpu.VMEM((4 * len(BASIS), *tile), F32),
             pltpu.VMEM((4 * MROWS, 256), F32),
             pltpu.VMEM((4 * MROWS, 256), F32),
             pltpu.VMEM((LANES, 26 * 256), BF16),
@@ -788,12 +853,12 @@
             pltpu.VMEM((LANES, 7 * LANES), BF16),
             pltpu.VMEM((LANES, 2 * LANES), BF16),
             pltpu.VMEM((16, 8 * LANES), BF16),
-            pltpu.VMEM((3, ROWS, 256), F32),
+            pltpu.VMEM((3, ROWS, LANES), F32),
             pltpu.VMEM((2, *tile), F32),
         ],
         compiler_params=pltpu.CompilerParams(collective_id=0, has_side_effects=True),
         name="whole_step",
-    )(*inputs)
+    )(*inputs, live, count)
     outs = [in_place(x) for x in outs]
     outs = pl.pallas_call(
         finish,

time: 23.3 us -> 22.4 us (0.961)
  Pallas kernels: 21.2 us -> 20.4 us
    pallas_call x1, Pallas kernels: 20.6 us -> 19.8 us  [whole_step(): pl.pallas_call(functools.partial(kernel, n_shock, n_trans), out_shape=tup...]
where the time goes in v4:
time: 22.4 us; the launch traced here: 22.3 us
  Pallas kernels  20.4 us (91%)
  between operations  1.94 us (9%)
    pallas_call x1, Pallas kernels, whole_step(): pl.pallas_call(functools.partial(kernel, n_shock, n_trans), out_shape=tup...  19.8 us
    pallas_call x1, Pallas kernels, whole_step(): pl.pallas_call(finish, out_shape=tuple((jax.ShapeDtypeStruct(shape, F32)...  0.61 us

profile of v4, /device:TPU:96, one launch (start us, length us, event | category | flops | bytes accessed | tf_op | source)
XLA Modules:
  0.0 22.3 jit_solution(16025617875404520428)
XLA Ops:
  1.9 19.8 %whole_step.1 = (f32[3,256]{1,0:T(4,128)S(1)}, f32[3,256]{1,0:T(4,128)S(1)}, f32[3,256]{1,0:T(4,128)S(1)}, f32[1,256]{1,0:T(1,128)S(1)}, f32[3,3,16]{2,1,0:T(4,128)S(1)}) custom-call(f32[3,256]{1,0:T(4,128)} %refs_0_.1, f32[3,256]{1,0:T(4,128)} %refs_1_.1, f32[3,256]{1,0:T(4,128)} %refs_2_.1, f32[1,50]{1,0:T(1,128)} %bitcast.3, f32[50,50]{1,0:T(8,128)} %refs_4_.1, ...), custom_call_target="tpu_custom_call" | custom-call | tf_op jit(solution)/shard_map/whole_step/pallas_call | solution.py:814
  21.7 0.6 %finish.1 = (f32[3,256]{1,0:T(4,128)}, f32[3,256]{1,0:T(4,128)}, f32[3,256]{1,0:T(4,128)}, f32[1,256]{1,0:T(1,128)}, f32[3,3,16]{2,1,0:T(4,128)}) custom-call(f32[3,256]{1,0:T(4,128)S(1)} %get-tuple-element.15.refs_0_, f32[3,256]{1,0:T(4,128)S(1)} %get-tuple-element.16.refs_1_, f32[3,256]{1,0:T(4,128)S(1)} %get-tuple-element.17.refs_2_, ...), custom_call_target="tpu_custom_call" | custom-call | tf_op jit(solution)/shard_map/finish/pallas_call | solution.py:863

commit v5 on v4

--- a/solution.py
+++ b/solution.py
@@ -19,10 +19,11 @@
 radial_width = 0.35
 radial_centers = (1.4, 1.9, 2.4, 2.9)
 moment_scale = 0.25
+spacing = radial_centers[1] - radial_centers[0]
 pair_list = ((0, 0), (0, 1), (0, 2), (0, 3), (1, 1), (1, 2), (1, 3), (2, 2), (2, 3), (3, 3))
 LANES = 128
 ROWS = 56
-CHUNKS = ((0, 16), (16, 32), (32, 48), (48, 56))
+CHUNKS = ((0, 8), (8, 16), (16, 32), (32, 48), (48, 56))
 MROWS = 40
 DROWS = 64
 
@@ -72,14 +73,23 @@
     return np.broadcast_to(table[:, :, None], (3, ROWS, LANES)).copy()
 
 
-def contraction_table():
+def multiplicity(t):
+    p, q, w = t
+    return math.factorial(p + q + w) / (math.factorial(p) * math.factorial(q) * math.factorial(w))
+
+
+def weight_rows():
+    rows = np.zeros((MROWS, 2 * LANES), dtype=np.float32)
+    for m, t in enumerate(TRIPLES):
+        rows[m] = multiplicity(t)
+    return rows
+
+
+def selection_table():
     table = np.zeros((DROWS, len(pair_list) * MROWS), dtype=np.float32)
     for i in range(len(pair_list)):
-        for m, (p, q, w) in enumerate(TRIPLES):
-            degree = p + q + w
-            table[5 * i + degree, MROWS * i + m] = math.factorial(degree) / (
-                math.factorial(p) * math.factorial(q) * math.factorial(w)
-            )
+        for m, t in enumerate(TRIPLES):
+            table[5 * i + sum(t), MROWS * i + m] = 1.0
     return table
 
 
@@ -186,8 +196,8 @@
         nb_lane,
         leave_idx,
         offs,
-        wmat,
-        wmat_t,
+        weight,
+        chosen,
         in_sems,
         t_send,
         s_send,
@@ -215,6 +225,8 @@
         tiles,
         mom,
         dmom,
+        mixing,
+        by_descriptor,
         onehot,
         apad,
         hot0,
@@ -235,8 +247,8 @@
         nb_lane,
         leave_idx,
         offs,
-        wmat,
-        wmat_t,
+        weight,
+        chosen,
     )
     loads = [
         pltpu.make_async_copy(src, dst, in_sems.at[i])
@@ -394,14 +406,14 @@
         ext[h, 0:3, :] = displaced[:, h * LANES : (h + 1) * LANES]
     idx_pad[0:1, 0:32] = trans_idx[1:2, :]
     idx_pad[1:2, 0:32] = trans_idx[0:1, :]
-    idx_pad[2:4, :] = shock_idx[...]
+    idx_pad[2:4, :] = pltpu.roll(shock_idx[...], 64, 1)
     t_row = jnp.where(lane_row < 32, idx_pad[0:1, :], pltpu.roll(idx_pad[1:2, :], 32, 1))
     shock8 = jnp.where(sub8 < 4, rows_of(idx_pad[2:3, :], 8), rows_of(idx_pad[3:4, :], 8))
     shock_block = shock8 >> 7
     shock_lane = shock8 & 127
     doubled = [jnp.where(sub8 < 4, ext[b], pltpu.roll(ext[b], 4, 0)) for b in range(2)]
     t_send[...] = lane_gather(ext[0], rows_of(t_row, 8))
-    t_send[4:6, :] = shock_idx[...].astype(F32)
+    t_send[4:6, :] = idx_pad[2:4, :].astype(F32)
     s_own = jnp.where(
         shock_block == 0,
         lane_gather(doubled[0], shock_lane),
@@ -469,6 +481,10 @@
     apad[0:50, 0:50] = alpha[...]
     sym = 0.5 * (apad[...] + apad[...].T)
     sym_hi, sym_lo = split(sym[0:DROWS, 0:DROWS])
+    mixed_hi, mixed_lo = split(mm(sym_hi, chosen[...]) + mm(sym_lo, chosen[...]))
+    mixing[0:DROWS, :] = mixed_lo
+    mixing[DROWS : 2 * DROWS, :] = mixed_hi
+    mixing[2 * DROWS : 3 * DROWS, :] = chosen[...]
     apad[0:1, :] = jnp.zeros((1, LANES), F32)
     apad[0:1, 0:50] = beta[...]
     beta_col = rows_of(apad[0:1, :], LANES).T[0:DROWS, :]
@@ -493,10 +509,9 @@
     )
     direct = jnp.where(sub8 < 4, pltpu.roll(from_low, 4, 0), pltpu.roll(from_up, 4, 0))
     both = jnp.where(lists >= 256, lane_gather(across, lists & 127), direct)
-    turned = pltpu.roll(both, 64, 1)
-    swapped = pltpu.roll(turned, 4, 0)
-    ext[2] = jnp.where(lane8 < 64, t_ghost, turned)
-    ext[3] = jnp.where(lane8 < 64, turned, swapped)
+    swapped = pltpu.roll(both, 4, 0)
+    ext[2] = jnp.where(lane8 < 64, t_ghost, both)
+    ext[3] = jnp.where(lane8 < 64, both, swapped)
     ext[4] = swapped
 
     table = jnp.where(
@@ -527,21 +542,20 @@
     ux, uy, uz = px * inverse, py * inverse, pz * inverse
     angle = (0.5 * math.pi) - (0.5 * math.pi / cutoff_radius) * distance
     sine, cosine = sin_of(angle), cos_of(angle)
-    scale = jnp.where(block >= 0, moment_scale, 0.0)
-    smooth = scale * sine * sine
-    slope = scale * (-math.pi / cutoff_radius) * sine * cosine
+    sine_live = jnp.where(block >= 0, moment_scale * sine, 0.0)
+    first_z = (distance - radial_centers[0]) * (1.0 / radial_width)
     radial = []
     for n, center in enumerate(radial_centers):
         z = (distance - center) * (1.0 / radial_width)
-        e = jnp.exp(-(z * z))
-        r = smooth * e
-        radial.append(r)
-        geom[n] = r
-        geom[4 + n] = slope * e - (2.0 / radial_width) * z * r
+        weighted = sine_live * jnp.exp(-(z * z))
+        radial.append(sine * weighted)
+        geom[n] = weighted
+    geom[4] = (-math.pi / cutoff_radius) * cosine - (2.0 / radial_width) * first_z * sine
+    geom[5] = (2.0 * spacing / radial_width**2) * sine
+    geom[6] = sine * inverse
     geom[8] = ux
     geom[9] = uy
     geom[10] = uz
-    geom[11] = inverse
     values = {}
     sums = {}
     for t in TRIPLES:
@@ -570,28 +584,38 @@
             mom[at : at + 1, LANES:] = sums[(n, t)][1:2, :]
 
     moments = [mom[n * MROWS : (n + 1) * MROWS, :] for n in range(4)]
-    products = jnp.concatenate([moments[n] * moments[o] for n, o in pair_list], axis=0)
+    heavy = [weight[...] * value for value in moments]
+    products = jnp.concatenate([moments[n] * heavy[o] for n, o in pair_list], axis=0)
     prod_hi, prod_lo = split(products)
-    weights = wmat[...]
-    descriptor = mm(weights, prod_hi) + mm(weights, prod_lo)
-    desc_hi, desc_lo = split(descriptor)
-    quadratic = mm(sym_hi, desc_hi) + mm(sym_lo, desc_hi) + mm(sym_hi, desc_lo)
-    energy = jnp.sum(descriptor * (beta_col + 0.5 * quadratic), axis=0, keepdims=True)
-    slope_hi, slope_lo = split(beta_col + quadratic)
-    weights_t = wmat_t[...]
-    dproducts = mm(weights_t, slope_hi) + mm(weights_t, slope_lo)
+    high = mm(mixing[...], prod_hi)
+    low = mm(mixing[DROWS : 3 * DROWS, :], prod_lo)
+    by_descriptor[...] = beta_col + (
+        high[0:DROWS, :] + high[DROWS : 2 * DROWS, :] + low[0:DROWS, :]
+    )
+    descriptor = high[2 * DROWS : 3 * DROWS, :] + low[DROWS : 2 * DROWS, :]
+    energy = 0.5 * jnp.sum(descriptor * (beta_col + by_descriptor[...]), axis=0, keepdims=True)
+    sub_wide = lax.broadcasted_iota(jnp.int32, (8, 2 * LANES), 0)
+    totals = [None] * 4
+    for i, (a, b) in enumerate(pair_list):
+        r = [rows_of(by_descriptor[5 * i + l : 5 * i + l + 1, :], 8) for l in range(5)]
+        spread_rows = jnp.concatenate(
+            [
+                jnp.where(sub_wide < 1, r[0], jnp.where(sub_wide < 4, r[1], r[2])),
+                jnp.where(sub_wide < 2, r[2], r[3]),
+                jnp.where(sub_wide < 4, r[3], r[4]),
+                r[4],
+                r[4],
+            ],
+            axis=0,
+        )
+        if a == b:
+            terms = ((a, 2.0 * spread_rows * heavy[a]),)
+        else:
+            terms = ((a, spread_rows * heavy[b]), (b, spread_rows * heavy[a]))
+        for n, term in terms:
+            totals[n] = term if totals[n] is None else totals[n] + term
     for n in range(4):
-        total = None
-        for i, (a, b) in enumerate(pair_list):
-            if n not in (a, b):
-                continue
-            part = dproducts[i * MROWS : (i + 1) * MROWS, :]
-            if a == b:
-                part = 2.0 * part * moments[n]
-            else:
-                part = part * moments[b if n == a else a]
-            total = part if total is None else total + part
-        dmom[n * MROWS : (n + 1) * MROWS, :] = total
+        dmom[n * MROWS : (n + 1) * MROWS, :] = totals[n]
 
     for n in range(4):
         slopes = {}
@@ -613,46 +637,43 @@
 
     part8 = sub8 & 3
     half_block = sub8 >> 2
-    spread = jnp.zeros((48, LANES), F32)
     own_total = [None] * 3
-    for begin, end in CHUNKS:
+
+    def pair_gradients(begin, end):
         count = (end - begin) // 8
         at = slice(begin, end)
-        radial = [geom[n, at, :] for n in range(4)]
+        weighted = [geom[n, at, :] for n in range(4)]
         unit = [geom[8 + c, at, :] for c in range(3)]
         ux, uy, uz = unit
         found = []
         for w in range(2):
             size = 4 - w
-            value_x = slope_x = slope_y = None
-            heights = [None] * 4
+            value_x = slope_x = slope_y = graded_x = None
             for p in range(size, -1, -1):
-                value = slope = None
-                rows = [None] * 4
+                value = slope = graded = None
                 for q in range(size - p, -1, -1):
-                    coefficient = None
-                    for n in range(4):
+                    total = graded_total = None
+                    for n in range(3, -1, -1):
                         b = over(tiles[n * len(BASIS) + PLACE[(p, q, w)]], count)
-                        rows[n] = b if rows[n] is None else rows[n] * uy + b
-                        term = b * radial[n]
-                        coefficient = term if coefficient is None else coefficient + term
-                    value, slope = horner(uy, value, slope, coefficient)
-                for n in range(4):
-                    heights[n] = rows[n] if heights[n] is None else heights[n] * ux + rows[n]
+                        term = b * weighted[n]
+                        total = term if total is None else total + term
+                        if n > 0:
+                            graded_total = total if graded_total is None else graded_total + total
+                    value, slope = horner(uy, value, slope, total)
+                    graded = graded_total if graded is None else graded * uy + graded_total
                 value_x, slope_x = horner(ux, value_x, slope_x, value)
+                graded_x = graded if graded_x is None else graded_x * ux + graded
                 if slope is not None:
                     slope_y = slope if slope_y is None else slope_y * ux + slope
-            found.append((value_x, slope_x, slope_y, heights))
-        inverse = geom[11, at, :]
+            found.append((value_x, slope_x, slope_y, graded_x))
+        scaled = geom[6, at, :]
         tangent = [
-            (found[0][1] + uz * found[1][1]) * inverse,
-            (found[0][2] + uz * found[1][2]) * inverse,
-            found[1][0] * inverse,
+            (found[0][1] + uz * found[1][1]) * scaled,
+            (found[0][2] + uz * found[1][2]) * scaled,
+            found[1][0] * scaled,
         ]
-        along = None
-        for n in range(4):
-            term = geom[4 + n, at, :] * (found[0][3][n] + uz * found[1][3][n])
-            along = term if along is None else along + term
+        along = geom[4, at, :] * (found[0][0] + uz * found[1][0])
+        along = along + geom[5, at, :] * (found[0][3] + uz * found[1][3])
         along = along - (ux * tangent[0] + uy * tangent[1] + uz * tangent[2])
         for c in range(3):
             g = tangent[c] + unit[c] * along
@@ -660,6 +681,8 @@
             for i in range(count):
                 row = g[8 * i : 8 * i + 8, :]
                 own_total[c] = row if own_total[c] is None else own_total[c] + row
+
+    def spread_sums(begin, end):
         columns = []
         for r in range(begin, min(end, 52)):
             gx, gy, gz = (rows_of(grads[c, r : r + 1, :], 8) for c in range(3))
@@ -674,9 +697,14 @@
                 ).astype(BF16)
             )
         last = min(end, 52)
-        spread = spread + mm_nt(
-            jnp.concatenate(columns, axis=1), onehot[:, begin * LANES : last * LANES]
-        )
+        return mm_nt(jnp.concatenate(columns, axis=1), onehot[:, begin * LANES : last * LANES])
+
+    spread = jnp.zeros((48, LANES), F32)
+    pair_gradients(*CHUNKS[0])
+    for at in range(len(CHUNKS)):
+        if at + 1 < len(CHUNKS):
+            pair_gradients(*CHUNKS[at + 1])
+        spread = spread + spread_sums(*CHUNKS[at])
     for c in range(3):
         total = own_total[c] + pltpu.roll(own_total[c], 4, 0)
         total = total + pltpu.roll(total, 2, 0)
@@ -686,14 +714,10 @@
     first = spread[0:8, :]
     second = spread[8:16, :]
     third = spread[16:24, :]
-    second_turned = pltpu.roll(second, 64, 1)
-    third_turned = pltpu.roll(third, 64, 1)
-    shifted = jnp.where(
-        sub8 < 4, pltpu.roll(second_turned, 4, 0), pltpu.roll(third_turned, 4, 0)
-    )
+    shifted = jnp.where(sub8 < 4, pltpu.roll(second, 4, 0), pltpu.roll(third, 4, 0))
     grad0 = first - own_sum[0]
     m_send[1] = second
-    m_send[0] = jnp.where(lane8 < 64, second_turned, shifted)
+    m_send[0] = jnp.where(lane8 < 64, shifted, second)
     p_send[...] = jnp.where(sub8 < 3, grad0, 0.0)
     start(backward)
     start(extra[1:3])
@@ -792,7 +816,6 @@
 
 def whole_step(n_shock, n_trans, *args):
     (disp, vel, force, beta, alpha, live, trans_idx, shock_idx, block, lane, leave, count) = args
-    table = contraction_table()
     inputs = (
         disp,
         vel,
@@ -805,8 +828,8 @@
         lane,
         leave.reshape(1, 16),
         jnp.asarray(lattice_rows()),
-        jnp.asarray(table, BF16),
-        jnp.asarray(table.T, BF16),
+        jnp.asarray(weight_rows()),
+        jnp.asarray(selection_table(), BF16),
     )
     vmem = pl.BlockSpec(memory_space=pltpu.VMEM)
     tile = (8, LANES)
@@ -844,10 +867,12 @@
             pltpu.VMEM((ROWS, LANES), jnp.int32),
             pltpu.VMEM(tile, jnp.int32),
             pltpu.VMEM((3, ROWS, LANES), F32),
-            pltpu.VMEM((12, ROWS, LANES), F32),
+            pltpu.VMEM((11, ROWS, LANES), F32),
             pltpu.VMEM((4 * len(BASIS), *tile), F32),
             pltpu.VMEM((4 * MROWS, 256), F32),
             pltpu.VMEM((4 * MROWS, 256), F32),
+            pltpu.VMEM((3 * DROWS, 10 * MROWS), BF16),
+            pltpu.VMEM((DROWS, 256), F32),
             pltpu.VMEM((LANES, 26 * 256), BF16),
             pltpu.VMEM((LANES, LANES), F32),
             pltpu.VMEM((LANES, 7 * LANES), BF16),

time: 22.4 us -> 22 us (0.982)
  Pallas kernels: 20.4 us -> 19.9 us
    pallas_call x1, Pallas kernels: 19.8 us -> 19.3 us  [whole_step(): pl.pallas_call(functools.partial(kernel, n_shock, n_trans), out_shape=tup...]
where the time goes in v5:
time: 22 us; the launch traced here: 21.9 us
  Pallas kernels  19.9 us (90%)
  between operations  1.94 us (9%)
    pallas_call x1, Pallas kernels, whole_step(): pl.pallas_call(functools.partial(kernel, n_shock, n_trans), out_shape=tup...  19.3 us
    pallas_call x1, Pallas kernels, whole_step(): pl.pallas_call(finish, out_shape=tuple((jax.ShapeDtypeStruct(shape, F32)...  0.61 us

profile of v5, /device:TPU:96, one launch (start us, length us, event | category | flops | bytes accessed | tf_op | source)
XLA Modules:
  0.0 21.9 jit_solution(17700504528769642474)
XLA Ops:
  1.9 19.3 %whole_step.1 = (f32[3,256]{1,0:T(4,128)S(1)}, f32[3,256]{1,0:T(4,128)S(1)}, f32[3,256]{1,0:T(4,128)S(1)}, f32[1,256]{1,0:T(1,128)S(1)}, f32[3,3,16]{2,1,0:T(4,128)S(1)}) custom-call(f32[3,256]{1,0:T(4,128)} %refs_0_.1, f32[3,256]{1,0:T(4,128)} %refs_1_.1, f32[3,256]{1,0:T(4,128)} %refs_2_.1, f32[1,50]{1,0:T(1,128)} %bitcast.3, f32[50,50]{1,0:T(8,128)} %refs_4_.1, ...), custom_call_target="tpu_custom_call" | custom-call | tf_op jit(solution)/shard_map/whole_step/pallas_call | solution.py:837
  21.2 0.6 %finish.1 = (f32[3,256]{1,0:T(4,128)}, f32[3,256]{1,0:T(4,128)}, f32[3,256]{1,0:T(4,128)}, f32[1,256]{1,0:T(1,128)}, f32[3,3,16]{2,1,0:T(4,128)}) custom-call(f32[3,256]{1,0:T(4,128)S(1)} %get-tuple-element.15.refs_0_, f32[3,256]{1,0:T(4,128)S(1)} %get-tuple-element.16.refs_1_, f32[3,256]{1,0:T(4,128)S(1)} %get-tuple-element.17.refs_2_, ...), custom_call_target="tpu_custom_call" | custom-call | tf_op jit(solution)/shard_map/finish/pallas_call | solution.py:888

commit v6 on v5

--- a/solution.py
+++ b/solution.py
@@ -220,6 +220,7 @@
         blk,
         lan,
         idx_pad,
+        joined,
         near_own,
         geom,
         tiles,
@@ -284,13 +285,13 @@
         def action():
             for dt in (-1, 0, 1):
                 k = DIRS.index((-ds, -dt))
-                b_recv[k] = jnp.zeros((2, 8, LANES), F32)
+                b_recv[k] = jnp.zeros((2, 4, LANES), F32)
                 if k < NEAR:
-                    f_recv[k] = jnp.zeros((8, LANES), F32)
+                    f_recv[k] = jnp.zeros((2, 4, LANES), F32)
             if ds == 1:
                 w_recv[...] = jnp.zeros((8, LANES), F32)
                 c_recv[...] = jnp.zeros((8, LANES), F32)
-                p_recv[...] = jnp.zeros((8, LANES), F32)
+                p_recv[...] = jnp.zeros((4, LANES), F32)
 
         pl.when(jnp.logical_not(inside[ds]))(action)
 
@@ -328,8 +329,8 @@
         (
             ds,
             remote(
-                s_send if dt == 0 else t_send,
-                f_recv.at[k],
+                s_send.at[(1 + ds) // 2] if dt == 0 else t_send if ds == 0 else t_send.at[0],
+                f_recv.at[k] if ds == 0 else f_recv.at[k, 0],
                 f_send_sems.at[k],
                 f_recv_sems.at[k],
                 (ds, dt),
@@ -341,15 +342,23 @@
         (
             ds,
             remote(
-                m_send if whole else m_send.at[0],
-                b_recv.at[k] if whole else b_recv.at[k, 0],
+                m_send.at[part],
+                b_recv.at[k, 0] if isinstance(part, int) else b_recv.at[k],
                 b_send_sems.at[k],
                 b_recv_sems.at[k],
                 (ds, dt),
             ),
         )
         for k, (ds, dt) in enumerate(DIRS)
-        for whole in (dt != 0 and ds in (0, -1),)
+        for part in (
+            0
+            if ds == 1
+            else pl.ds(0, 2)
+            if ds == 0
+            else pl.ds(1, 2)
+            if ds == -1 and dt != 0
+            else 2,
+        )
     ]
     extra = [
         (-1, remote(src, dst, x_send_sems.at[i], x_recv_sems.at[i], (-1, 0)))
@@ -397,6 +406,7 @@
     sub8 = lax.broadcasted_iota(jnp.int32, (8, LANES), 0)
 
     idx_pad[...] = jnp.zeros_like(idx_pad)
+    joined[...] = jnp.zeros_like(joined)
     ext[...] = jnp.zeros_like(ext)
     for i in (0, 1, 2, 5, 6):
         loads[i].wait()
@@ -412,14 +422,17 @@
     shock_block = shock8 >> 7
     shock_lane = shock8 & 127
     doubled = [jnp.where(sub8 < 4, ext[b], pltpu.roll(ext[b], 4, 0)) for b in range(2)]
-    t_send[...] = lane_gather(ext[0], rows_of(t_row, 8))
-    t_send[4:6, :] = idx_pad[2:4, :].astype(F32)
+    t_send[0] = lane_gather(ext[0], rows_of(t_row, 8))[0:4, :]
+    t_send[1] = jnp.zeros((4, LANES), F32)
+    t_send[1, 0:2, :] = idx_pad[2:4, :].astype(F32)
     s_own = jnp.where(
         shock_block == 0,
         lane_gather(doubled[0], shock_lane),
         jnp.where(shock_block == 1, lane_gather(doubled[1], shock_lane), 0.0),
     )
-    s_send[...] = jnp.where((sub8 & 3) == 3, shock8.astype(F32), s_own)
+    s_all = jnp.where((sub8 & 3) == 3, shock8.astype(F32), s_own)
+    s_send[0] = s_all[0:4, :]
+    s_send[1] = s_all[4:8, :]
 
     pl.semaphore_wait(barrier, peers)
     start(forward)
@@ -494,29 +507,30 @@
 
     receive(forward)
 
+    lane4 = lane8[0:4, :]
+
     def between(lower, upper):
-        return jnp.where(lane8 < 32, lower, jnp.where(lane8 < 64, upper, 0.0))
-
-    t_ghost = between(f_recv[slot(0, -1)], f_recv[slot(0, 1)])
-    from_low = f_recv[slot(-1, 0)]
-    from_up = f_recv[slot(1, 0)]
-    lists = jnp.where(sub8 < 4, rows_of(from_low[7:8, :], 8), rows_of(from_up[3:4, :], 8))
+        return jnp.where(lane4 < 32, lower, jnp.where(lane4 < 64, upper, 0.0))
+
+    joined[0, 0:4, :] = between(f_recv[slot(-1, -1), 0], f_recv[slot(-1, 1), 0])
+    joined[0, 4:8, :] = between(f_recv[slot(1, -1), 0], f_recv[slot(1, 1), 0])
+    joined[1, 0:4, :] = f_recv[slot(-1, 0), 0]
+    joined[1, 4:8, :] = f_recv[slot(1, 0), 0]
+    joined[2, 0:4, :] = between(f_recv[slot(0, -1), 0], f_recv[slot(0, 1), 0])
+    joined[3, 2:4, :] = f_recv[slot(0, 1), 1][0:2, :]
+    joined[3, 4:6, :] = f_recv[slot(0, -1), 1][0:2, :]
+    across = joined[0]
+    direct = joined[1]
+    t_ghost = joined[2]
+    lists = jnp.where(sub8 < 4, rows_of(direct[3:4, :], 8), rows_of(direct[7:8, :], 8))
     lists = lists.astype(jnp.int32)
-    across = jnp.where(
-        sub8 < 4,
-        between(f_recv[slot(-1, -1)], f_recv[slot(-1, 1)]),
-        pltpu.roll(between(f_recv[slot(1, -1)], f_recv[slot(1, 1)]), 4, 0),
-    )
-    direct = jnp.where(sub8 < 4, pltpu.roll(from_low, 4, 0), pltpu.roll(from_up, 4, 0))
     both = jnp.where(lists >= 256, lane_gather(across, lists & 127), direct)
     swapped = pltpu.roll(both, 4, 0)
     ext[2] = jnp.where(lane8 < 64, t_ghost, both)
     ext[3] = jnp.where(lane8 < 64, both, swapped)
     ext[4] = swapped
 
-    table = jnp.where(
-        sub8 < 4, pltpu.roll(f_recv[slot(0, 1)], 6, 0), f_recv[slot(0, -1)]
-    ).astype(jnp.int32)
+    table = joined[3].astype(jnp.int32)
     through = lane_gather(rows_of(t_row, 8), table & 127)
     first_of = jnp.where(sub8 < 4, 256, 288)
     through = jnp.where(table >= first_of, jnp.where(table < first_of + 32, through, -1), -1)
@@ -714,11 +728,12 @@
     first = spread[0:8, :]
     second = spread[8:16, :]
     third = spread[16:24, :]
-    shifted = jnp.where(sub8 < 4, pltpu.roll(second, 4, 0), pltpu.roll(third, 4, 0))
+    swapped = pltpu.roll(second, 4, 0)
     grad0 = first - own_sum[0]
-    m_send[1] = second
-    m_send[0] = jnp.where(lane8 < 64, shifted, second)
-    p_send[...] = jnp.where(sub8 < 3, grad0, 0.0)
+    m_send[0] = jnp.where(lane8 < 64, third, swapped)[0:4, :]
+    m_send[1] = second[0:4, :]
+    m_send[2] = jnp.where(lane8 < 64, swapped, second)[0:4, :]
+    p_send[...] = jnp.where(sub8 < 3, grad0, 0.0)[0:4, :]
     start(backward)
     start(extra[1:3])
 
@@ -745,48 +760,45 @@
     receive(backward)
     receive(extra[2:3])
 
-    def lower_of(ds, dt):
-        return b_recv[slot(ds, dt), 0]
-
-    def upper_of(ds, dt):
-        return pltpu.roll(b_recv[slot(ds, dt), 0], 4, 0)
+    def piece(ds, dt, part=0):
+        return b_recv[slot(ds, dt), part]
 
     def pieces_of(tiles):
-        back = jnp.concatenate([jnp.where(sub8 < 3, tile, 0.0) for tile in tiles], axis=1)
+        back = jnp.concatenate(tiles, axis=1)
         hi = back.astype(BF16).astype(F32)
         return jnp.concatenate([hi, back - hi], axis=0).astype(BF16)
 
     back = pieces_of(
         (
-            upper_of(-1, 0),
-            lower_of(1, 0),
-            upper_of(-1, 1),
-            lower_of(1, 1),
-            upper_of(-1, -1),
-            lower_of(1, -1),
-            between(b_recv[slot(0, 1), 1], b_recv[slot(0, -1), 1]),
+            piece(-1, 0),
+            piece(1, 0),
+            piece(-1, 1),
+            piece(1, 1, 1),
+            piece(-1, -1),
+            piece(1, -1, 1),
+            between(piece(0, 1, 1), piece(0, -1, 1)),
         )
     )
     added0 = mm_nt(back, hot0[...])
     added1 = mm_nt(back[:, 0 : 2 * LANES], hot1[...])
     arriving = pieces_of(
         (
-            pltpu.roll(m_send[0], 4, 0),
-            lower_of(2, 0),
-            upper_of(0, 1),
-            lower_of(2, 1),
-            upper_of(0, -1),
-            lower_of(2, -1),
-            between(b_recv[slot(1, 1), 1], b_recv[slot(1, -1), 1]),
+            m_send[0],
+            piece(2, 0),
+            piece(0, 1),
+            piece(2, 1),
+            piece(0, -1),
+            piece(2, -1),
+            between(piece(1, 1), piece(1, -1)),
             p_recv[...],
         )
     )
     added2 = mm_nt(arriving, arr_hot[...])
-    force0 = -(grad0 + added0[0:8, :] + added0[8:16, :])[0:3, :]
+    force0 = -(grad0 + added0 + pltpu.roll(added0, 4, 0))[0:3, :]
     velocity0 = half_velocity[:, 0:LANES] + kick_factor * force0
-    force1 = -(grad1 + added1[0:8, :] + added1[8:16, :])[0:3, :]
+    force1 = -(grad1 + added1 + pltpu.roll(added1, 4, 0))[0:3, :]
     velocity1 = half_velocity[:, LANES:] + kick_factor * force1
-    force2 = -(added2[0:8, :] + added2[8:16, :])[0:3, :]
+    force2 = -(added2 + pltpu.roll(added2, 4, 0))[0:3, :]
     state = w_recv[...]
     out_vel[:, 0:LANES] = velocity0 * rows_of(keep0, 3)
     out_force[:, 0:LANES] = force0 * rows_of(keep0, 3)
@@ -833,6 +845,7 @@
     )
     vmem = pl.BlockSpec(memory_space=pltpu.VMEM)
     tile = (8, LANES)
+    half_tile = (4, LANES)
     shapes = ((3, 256), (3, 256), (3, 256), (1, 256), (3, 3, 16))
     outs = pl.pallas_call(
         functools.partial(kernel, n_shock, n_trans),
@@ -845,17 +858,17 @@
         ]
         + [
             pltpu.SemaphoreType.DMA((N_IN,)),
-            pltpu.VMEM(tile, F32),
-            pltpu.VMEM(tile, F32),
-            pltpu.VMEM((NEAR, *tile), F32),
-            pltpu.VMEM((2, *tile), F32),
-            pltpu.VMEM((len(DIRS), 2, *tile), F32),
+            pltpu.VMEM((2, *half_tile), F32),
+            pltpu.VMEM((2, *half_tile), F32),
+            pltpu.VMEM((NEAR, 2, *half_tile), F32),
+            pltpu.VMEM((3, *half_tile), F32),
+            pltpu.VMEM((len(DIRS), 2, *half_tile), F32),
             pltpu.VMEM(tile, F32),
             pltpu.VMEM(tile, F32),
             pltpu.VMEM(tile, F32),
             pltpu.VMEM(tile, F32),
-            pltpu.VMEM(tile, F32),
-            pltpu.VMEM(tile, F32),
+            pltpu.VMEM(half_tile, F32),
+            pltpu.VMEM(half_tile, F32),
             pltpu.SemaphoreType.DMA((NEAR,)),
             pltpu.SemaphoreType.DMA((NEAR,)),
             pltpu.SemaphoreType.DMA((len(DIRS),)),
@@ -866,6 +879,7 @@
             pltpu.VMEM((ROWS, LANES), jnp.int32),
             pltpu.VMEM((ROWS, LANES), jnp.int32),
             pltpu.VMEM(tile, jnp.int32),
+            pltpu.VMEM((4, *tile), F32),
             pltpu.VMEM((3, ROWS, LANES), F32),
             pltpu.VMEM((11, ROWS, LANES), F32),
             pltpu.VMEM((4 * len(BASIS), *tile), F32),

time: 22 us -> 21.9 us (level)
  no operation moved by 1% of the time
where the time goes in v6:
time: 21.9 us; the launch traced here: 21.7 us
  Pallas kernels  19.8 us (90%)
  between operations  1.94 us (9%)
    pallas_call x1, Pallas kernels, whole_step(): pl.pallas_call(functools.partial(kernel, n_shock, n_trans), out_shape=tup...  19.2 us
    pallas_call x1, Pallas kernels, whole_step(): pl.pallas_call(finish, out_shape=tuple((jax.ShapeDtypeStruct(shape, F32)...  0.61 us

profile of v6, /device:TPU:96, one launch (start us, length us, event | category | flops | bytes accessed | tf_op | source)
XLA Modules:
  0.0 21.7 jit_solution(5327247163245395507)
XLA Ops:
  1.9 19.2 %whole_step.1 = (f32[3,256]{1,0:T(4,128)S(1)}, f32[3,256]{1,0:T(4,128)S(1)}, f32[3,256]{1,0:T(4,128)S(1)}, f32[1,256]{1,0:T(1,128)S(1)}, f32[3,3,16]{2,1,0:T(4,128)S(1)}) custom-call(f32[3,256]{1,0:T(4,128)} %refs_0_.1, f32[3,256]{1,0:T(4,128)} %refs_1_.1, f32[3,256]{1,0:T(4,128)} %refs_2_.1, f32[1,50]{1,0:T(1,128)} %bitcast.3, f32[50,50]{1,0:T(8,128)} %refs_4_.1, ...), custom_call_target="tpu_custom_call" | custom-call | tf_op jit(solution)/shard_map/whole_step/pallas_call | solution.py:850
  21.1 0.6 %finish.1 = (f32[3,256]{1,0:T(4,128)}, f32[3,256]{1,0:T(4,128)}, f32[3,256]{1,0:T(4,128)}, f32[1,256]{1,0:T(1,128)}, f32[3,3,16]{2,1,0:T(4,128)}) custom-call(f32[3,256]{1,0:T(4,128)S(1)} %get-tuple-element.15.refs_0_, f32[3,256]{1,0:T(4,128)S(1)} %get-tuple-element.16.refs_1_, f32[3,256]{1,0:T(4,128)S(1)} %get-tuple-element.17.refs_2_, ...), custom_call_target="tpu_custom_call" | custom-call | tf_op jit(solution)/shard_map/finish/pallas_call | solution.py:902

commit v7 on v6

--- a/solution.py
+++ b/solution.py
@@ -176,6 +176,7 @@
     (-2, -1),
     (-2, 0),
 )
+GROUPS = (1, -1, 0, -2)
 NEAR = 8
 N_IN = 13
 
@@ -210,12 +211,8 @@
         c_recv,
         p_send,
         p_recv,
-        f_send_sems,
-        f_recv_sems,
-        b_send_sems,
-        b_recv_sems,
-        x_send_sems,
-        x_recv_sems,
+        send_sems,
+        recv_sems,
         ext,
         blk,
         lan,
@@ -291,7 +288,7 @@
             if ds == 1:
                 w_recv[...] = jnp.zeros((8, LANES), F32)
                 c_recv[...] = jnp.zeros((8, LANES), F32)
-                p_recv[...] = jnp.zeros((4, LANES), F32)
+                p_recv[...] = jnp.zeros((8, LANES), F32)
 
         pl.when(jnp.logical_not(inside[ds]))(action)
 
@@ -331,8 +328,8 @@
             remote(
                 s_send.at[(1 + ds) // 2] if dt == 0 else t_send if ds == 0 else t_send.at[0],
                 f_recv.at[k] if ds == 0 else f_recv.at[k, 0],
-                f_send_sems.at[k],
-                f_recv_sems.at[k],
+                send_sems.at[GROUPS.index(ds)],
+                recv_sems.at[GROUPS.index(ds)],
                 (ds, dt),
             ),
         )
@@ -344,8 +341,8 @@
             remote(
                 m_send.at[part],
                 b_recv.at[k, 0] if isinstance(part, int) else b_recv.at[k],
-                b_send_sems.at[k],
-                b_recv_sems.at[k],
+                send_sems.at[GROUPS.index(ds)],
+                recv_sems.at[4 + GROUPS.index(ds)],
                 (ds, dt),
             ),
         )
@@ -361,7 +358,10 @@
         )
     ]
     extra = [
-        (-1, remote(src, dst, x_send_sems.at[i], x_recv_sems.at[i], (-1, 0)))
+        (
+            -1,
+            remote(src, dst, send_sems.at[GROUPS.index(-1)], recv_sems.at[(3, 3, 5)[i]], (-1, 0)),
+        )
         for i, (src, dst) in enumerate(((w_send, w_recv), (c_send, c_recv), (p_send, p_recv)))
     ]
 
@@ -376,27 +376,21 @@
             if chosen:
                 where_inside(ds, action)
 
-    def receive(copies):
-        for ds in (0, 1, -1, -2):
-            chosen = [copy for at, copy in copies if at == ds]
-
-            def action(chosen=chosen):
-                for copy in chosen:
-                    copy.wait_recv()
-
-            if chosen:
-                where_inside(-ds, action)
-
-    def drain(copies):
-        for ds in (0, 1, -1, -2):
-            chosen = [copy for at, copy in copies if at == ds]
-
-            def action(chosen=chosen):
-                for copy in chosen:
-                    copy.wait_send()
-
-            if chosen:
-                where_inside(ds, action)
+    def pieces(count):
+        if count > len(DIRS):
+            return b_recv.at[pl.ds(0, count // 2)]
+        return b_recv.at[pl.ds(0, count), 0]
+
+    def waited(count, k):
+        return remote(pieces(count), pieces(count), send_sems.at[k % 4], recv_sems.at[k], (0, 1))
+
+    def receive(counts):
+        for k, ds, count in counts:
+            where_inside(-ds, lambda k=k, count=count: waited(count, k).wait_recv())
+
+    def drain():
+        for k, (ds, count) in enumerate(zip(GROUPS, (6, 14, 8, 3), strict=True)):
+            where_inside(ds, lambda k=k, count=count: waited(count, k).wait_send())
 
     def slot(ds, dt):
         return DIRS.index((-ds, -dt))
@@ -505,7 +499,7 @@
     for n in range(4):
         mom[n * MROWS + 32 : (n + 1) * MROWS, :] = jnp.zeros((8, 2 * LANES), F32)
 
-    receive(forward)
+    receive(((2, 0, 4), (0, 1, 3), (1, -1, 3)))
 
     lane4 = lane8[0:4, :]
 
@@ -733,7 +727,7 @@
     m_send[0] = jnp.where(lane8 < 64, third, swapped)[0:4, :]
     m_send[1] = second[0:4, :]
     m_send[2] = jnp.where(lane8 < 64, swapped, second)[0:4, :]
-    p_send[...] = jnp.where(sub8 < 3, grad0, 0.0)[0:4, :]
+    p_send[...] = jnp.where(sub8 < 3, grad0, 0.0)
     start(backward)
     start(extra[1:3])
 
@@ -749,7 +743,7 @@
     out_energy[:, LANES:] = energy[:, LANES:] * keep1
     grad1 = pltpu.roll(first, 4, 0) - own_sum[1]
 
-    receive(extra[0:2])
+    receive(((3, -1, 4),))
     slots = rows_of(c_recv[7:8, :], LANES).T[0:16, :]
     for i in range(8):
         row = lane_row.astype(F32) if i == 7 else c_recv[i : i + 1, :]
@@ -757,8 +751,7 @@
             rows_of(row, 16) == slots, 1.0, 0.0
         ).astype(BF16)
 
-    receive(backward)
-    receive(extra[2:3])
+    receive(((6, 0, 4), (4, 1, 3), (5, -1, 7), (7, -2, 3)))
 
     def piece(ds, dt, part=0):
         return b_recv[slot(ds, dt), part]
@@ -790,7 +783,7 @@
             piece(0, -1),
             piece(2, -1),
             between(piece(1, 1), piece(1, -1)),
-            p_recv[...],
+            p_recv[0:4, :],
         )
     )
     added2 = mm_nt(arriving, arr_hot[...])
@@ -808,9 +801,7 @@
         (state[0:3, 0:16], state[4:7, 0:16] + kick_factor * force2, force2)
     ):
         out_arr[q] = jnp.where(s_me < n_shock - 1, value, 0.0)
-    drain(forward)
-    drain(backward)
-    drain(extra)
+    drain()
 
 
 def kept(shape):
@@ -867,14 +858,10 @@
             pltpu.VMEM(tile, F32),
             pltpu.VMEM(tile, F32),
             pltpu.VMEM(tile, F32),
-            pltpu.VMEM(half_tile, F32),
-            pltpu.VMEM(half_tile, F32),
-            pltpu.SemaphoreType.DMA((NEAR,)),
-            pltpu.SemaphoreType.DMA((NEAR,)),
-            pltpu.SemaphoreType.DMA((len(DIRS),)),
-            pltpu.SemaphoreType.DMA((len(DIRS),)),
-            pltpu.SemaphoreType.DMA((3,)),
-            pltpu.SemaphoreType.DMA((3,)),
+            pltpu.VMEM(tile, F32),
+            pltpu.VMEM(tile, F32),
+            pltpu.SemaphoreType.DMA((4,)),
+            pltpu.SemaphoreType.DMA((8,)),
             pltpu.VMEM((7, *tile), F32),
             pltpu.VMEM((ROWS, LANES), jnp.int32),
             pltpu.VMEM((ROWS, LANES), jnp.int32),

time: 21.9 us -> 21.5 us (0.982)
  Pallas kernels: 19.8 us -> 19.5 us
    pallas_call x1, Pallas kernels: 19.2 us -> 18.8 us  [whole_step(): pl.pallas_call(functools.partial(kernel, n_shock, n_trans), out_shape=tup...]
where the time goes in v7:
time: 21.5 us; the launch traced here: 21.4 us
  Pallas kernels  19.5 us (91%)
  between operations  1.94 us (9%)
    pallas_call x1, Pallas kernels, whole_step(): pl.pallas_call(functools.partial(kernel, n_shock, n_trans), out_shape=tup...  18.8 us
    pallas_call x1, Pallas kernels, whole_step(): pl.pallas_call(finish, out_shape=tuple((jax.ShapeDtypeStruct(shape, F32)...  0.61 us

profile of v7, /device:TPU:96, one launch (start us, length us, event | category | flops | bytes accessed | tf_op | source)
XLA Modules:
  0.0 21.4 jit_solution(14478615088320510963)
XLA Ops:
  1.9 18.8 %whole_step.1 = (f32[3,256]{1,0:T(4,128)S(1)}, f32[3,256]{1,0:T(4,128)S(1)}, f32[3,256]{1,0:T(4,128)S(1)}, f32[1,256]{1,0:T(1,128)S(1)}, f32[3,3,16]{2,1,0:T(4,128)S(1)}) custom-call(f32[3,256]{1,0:T(4,128)} %refs_0_.1, f32[3,256]{1,0:T(4,128)} %refs_1_.1, f32[3,256]{1,0:T(4,128)} %refs_2_.1, f32[1,50]{1,0:T(1,128)} %bitcast.3, f32[50,50]{1,0:T(8,128)} %refs_4_.1, ...), custom_call_target="tpu_custom_call" | custom-call | tf_op jit(solution)/shard_map/whole_step/pallas_call | solution.py:841
  20.8 0.6 %finish.1 = (f32[3,256]{1,0:T(4,128)}, f32[3,256]{1,0:T(4,128)}, f32[3,256]{1,0:T(4,128)}, f32[1,256]{1,0:T(1,128)}, f32[3,3,16]{2,1,0:T(4,128)}) custom-call(f32[3,256]{1,0:T(4,128)S(1)} %get-tuple-element.15.refs_0_, f32[3,256]{1,0:T(4,128)S(1)} %get-tuple-element.16.refs_1_, f32[3,256]{1,0:T(4,128)S(1)} %get-tuple-element.17.refs_2_, ...), custom_call_target="tpu_custom_call" | custom-call | tf_op jit(solution)/shard_map/finish/pallas_call | solution.py:889

commit v8 on v7

--- a/solution.py
+++ b/solution.py
@@ -429,7 +429,8 @@
     s_send[1] = s_all[4:8, :]
 
     pl.semaphore_wait(barrier, peers)
-    start(forward)
+    start(forward[0:6])
+    start(forward[6:8])
     for ds in (-1, 1, 2):
         clear(ds)
 
@@ -728,7 +729,8 @@
     m_send[1] = second[0:4, :]
     m_send[2] = jnp.where(lane8 < 64, swapped, second)[0:4, :]
     p_send[...] = jnp.where(sub8 < 3, grad0, 0.0)
-    start(backward)
+    start(backward[0:6] + backward[8:10])
+    start(backward[6:8] + backward[10:11])
     start(extra[1:3])
 
     rows = [c_send[i : i + 1, :].astype(jnp.int32) for i in range(7)]

time: 21.5 us -> 21.5 us (level)
  no operation moved by 1% of the time
where the time goes in v8:
time: 21.5 us; the launch traced here: 21.4 us
  Pallas kernels  19.4 us (90%)
  between operations  1.94 us (9%)
    pallas_call x1, Pallas kernels, whole_step(): pl.pallas_call(functools.partial(kernel, n_shock, n_trans), out_shape=tup...  18.8 us
    pallas_call x1, Pallas kernels, whole_step(): pl.pallas_call(finish, out_shape=tuple((jax.ShapeDtypeStruct(shape, F32)...  0.61 us

profile of v8, /device:TPU:96, one launch (start us, length us, event | category | flops | bytes accessed | tf_op | source)
XLA Modules:
  0.0 21.4 jit_solution(1394359085336879242)
XLA Ops:
  1.9 18.8 %whole_step.1 = (f32[3,256]{1,0:T(4,128)S(1)}, f32[3,256]{1,0:T(4,128)S(1)}, f32[3,256]{1,0:T(4,128)S(1)}, f32[1,256]{1,0:T(1,128)S(1)}, f32[3,3,16]{2,1,0:T(4,128)S(1)}) custom-call(f32[3,256]{1,0:T(4,128)} %refs_0_.1, f32[3,256]{1,0:T(4,128)} %refs_1_.1, f32[3,256]{1,0:T(4,128)} %refs_2_.1, f32[1,50]{1,0:T(1,128)} %bitcast.3, f32[50,50]{1,0:T(8,128)} %refs_4_.1, ...), custom_call_target="tpu_custom_call" | custom-call | tf_op jit(solution)/shard_map/whole_step/pallas_call | solution.py:843
  20.8 0.6 %finish.1 = (f32[3,256]{1,0:T(4,128)}, f32[3,256]{1,0:T(4,128)}, f32[3,256]{1,0:T(4,128)}, f32[1,256]{1,0:T(1,128)}, f32[3,3,16]{2,1,0:T(4,128)}) custom-call(f32[3,256]{1,0:T(4,128)S(1)} %get-tuple-element.15.refs_0_, f32[3,256]{1,0:T(4,128)S(1)} %get-tuple-element.16.refs_1_, f32[3,256]{1,0:T(4,128)S(1)} %get-tuple-element.17.refs_2_, ...), custom_call_target="tpu_custom_call" | custom-call | tf_op jit(solution)/shard_map/finish/pallas_call | solution.py:891
